TPU v7x, 256 devices: a whole 4x4x8 slice. The times are simulated.
256 devices in a mesh: grp: 8 (over y, core), dom: 32 (over z, x).
Axes of the slice: x: 4, y: 4, z: 8, core: 2. Of those that a mesh axis runs over, the one named last changes fastest.
Arguments:
- element_state: float32 [56, 9, 163840], P(None, None, ('grp', 'dom')), may hold values from -6 to 6
- stiffness: float32 [3, 56, 56], replicated, may hold values from -0.75 to 0.75
- flux_local: float32 [4, 56, 56], replicated, may hold values from -0.75 to 0.75
- flux_remote: float32 [4, 56, 56], replicated, may hold values from -0.75 to 0.75
- star_matrix: float32 [3, 9, 9, 163840], P(None, None, None, ('grp', 'dom')), may hold values from -0.18 to 0.18
- face_local: float32 [4, 9, 9, 163840], P(None, None, None, ('grp', 'dom')), may hold values from -0.15 to 0.15
- face_remote: float32 [4, 9, 9, 163840], P(None, None, None, ('grp', 'dom')), may hold values from -0.15 to 0.15
- energy_weight: float32 [9, 163840], P(None, ('grp', 'dom')), may hold values from 0.5 to 18
- face_neighbour: int32 [4, 163840], P(None, ('grp', 'dom')), may hold values from 0 to 1151, as said below
- element_count: int32 [256], P(('grp', 'dom')), may hold values from 160 to 640, as said below
- send_count: int32 [256, 8], P(('grp', 'dom')), may hold values from 0 to 64, as said below
- send_element: int32 [256, 8, 64], P(('grp', 'dom')), may hold values from 0 to 639, as said below
- receiver_element: int32 [4096], P(('grp', 'dom')), may hold values from 0 to 639, as said below
- receiver_slot: int32 [4096], P(('grp', 'dom')), may hold values from 0 to 511, as said below
- receiver_weight: float32 [56, 4096], P(None, ('grp', 'dom')), may hold values from -0.75 to 0.75
Outputs:
- new_state: float32 [56, 9, 163840], P(None, None, ('grp', 'dom'))
- energy: float32 [8, 3], P('grp')
- traces: float32 [3, 9, 4096], P(None, None, ('grp', 'dom'))
Inputs may be any that keep to these rules, and one draw needn't show every extreme that they name: The first element_count[p] slots of a partition are active. In every slab 4 partitions in a row along dom (cyclically) hold 640 active elements; the others hold from 160 to 320. `send_count`: every partition has exactly 64 in one of its first 6 slots. `send_element`: names active elements of the sending partition. `face_neighbour`: values below 640 name active elements of the partition itself. `receiver_element`: names an active element of the owning partition. `receiver_slot`: within each slab a permutation of the 512 rows.
All inputs are finite; a program needn't handle non-finite values.
Results may differ from a plain program's by a relative error of at most 0.0001.
Values sent between devices are 32-bit elements; how exact they have to be, the bound alone decides.
No kernel may reach another device: no remote copies, remote signals or barrier semaphores. Data moves between devices by JAX's collectives and lax.ppermute only.
A program may use at most 128 MiB of HBM per device.

v0:
```python
import jax
import jax.numpy as jnp
from jax import lax
from jax.experimental import pallas as pl
from jax.experimental.pallas import tpu as pltpu
from jax.sharding import PartitionSpec as P


PEER_REACH = 3
TIME_STEPS = 3
GRP_DOM = ("grp", "dom")
LANES = 128
HALF = 64
SEND_ROWS = 256
FIRST_SENDS = (6, 7, 0, 1, 5)
F32 = jnp.float32
BF16 = jnp.bfloat16
highest = lax.Precision.HIGHEST


def two_parts(value):
    high = value.astype(BF16)
    low = (value - high.astype(F32)).astype(BF16)
    return high, low


def dot(a, b):
    return jnp.dot(a, b, preferred_element_type=F32)


def padded_k(matrices):
    rounded = lax.reduce_precision(matrices, 8, 7)
    low = matrices - rounded
    total = jnp.zeros((matrices.shape[0], 3 * HALF), F32)
    for part, value in enumerate((rounded, rounded, low)):
        after = 3 * HALF - part * HALF - matrices.shape[1]
        total = total + jnp.pad(value, ((0, 0), (part * HALF, after)))
    return total.astype(BF16)


def stack_columns(field, rhs_ref):
    basis = field.shape[0]
    high, low = two_parts(field)
    rhs_ref[0:basis, :] = high
    rhs_ref[HALF : HALF + basis, :] = low
    rhs_ref[2 * HALF : 2 * HALF + basis, :] = high


def clear_fill(rhs_ref, basis):
    for part in range(3):
        rhs_ref[part * HALF + basis : (part + 1) * HALF, :] = jnp.zeros(
            (HALF - basis, rhs_ref.shape[1]), BF16
        )


def pick(field, chosen):
    high, low = two_parts(field)
    return dot(high, chosen) + dot(low, chosen)


def apply_maps(tile, matrices, base, emit, quantities, basis):
    lanes = pl.ds(pl.multiple_of(tile * LANES, LANES), LANES)
    group = 3
    for first in range(0, quantities, group):

        def column(q, total):
            total = list(total)
            rows = pl.ds(pl.multiple_of(q * basis, 8), basis)
            for ref, at, sign, terms_ref, slot in matrices:
                term = terms_ref[slot, rows, lanes]
                for k in range(group):
                    product = ref[first + k, q, at : at + 1, lanes] * term
                    total[k] = total[k] + product if sign > 0 else total[k] - product
            return tuple(total)

        start = tuple(base(first + k, lanes) for k in range(group))
        total = lax.fori_loop(0, quantities, column, start)
        for k in range(group):
            emit(first + k, lanes, total[k])


def pack(field, select_ref, weight_ref, message_refs, values_ref, quantities, basis):
    rows = quantities * basis
    lane = lax.broadcasted_iota(jnp.int32, (SEND_ROWS, LANES), 1) < HALF
    tail = SEND_ROWS - (rows - SEND_ROWS)
    pairs = len(message_refs) // 2
    receivers = weight_ref.shape[1]
    if not pairs:
        picked = pick(field, select_ref[:, select_ref.shape[1] - LANES :])
    else:
        picked = pick(field, select_ref[...])
    for pair in range(pairs):
        block = picked[:, pair * LANES : (pair + 1) * LANES]
        top = block[:SEND_ROWS]
        bottom = jnp.concatenate([block[SEND_ROWS:], jnp.zeros((tail, LANES), F32)], 0)
        message_refs[2 * pair][...] = jnp.where(lane, top, pltpu.roll(bottom, HALF, 1))
        message_refs[2 * pair + 1][...] = jnp.where(lane, pltpu.roll(top, HALF, 1), bottom)
    block = picked[:, pairs * LANES : pairs * LANES + receivers]
    for q in range(quantities):
        values_ref[q : q + 1, :] = jnp.sum(
            block[q * basis : (q + 1) * basis] * weight_ref[...], axis=0, keepdims=True
        )


def first_kernel(count_ref, field_ref, send_ref, receiver_ref, weight_ref, select_ref, *messages):
    rows, width = field_ref.shape
    basis = weight_ref.shape[0]
    slots, capacity = send_ref.shape
    receivers = receiver_ref.shape[1]
    select_ref[:, slots * capacity :] = jnp.zeros((width, LANES), BF16)
    element = lax.broadcasted_iota(jnp.int32, (width, capacity), 0)
    place = lax.broadcasted_iota(jnp.int32, (1, capacity), 1)
    for slot in range(slots):
        asked = jnp.where(place < count_ref[0, slot], send_ref[slot : slot + 1, :], -1)
        select_ref[:, slot * capacity : (slot + 1) * capacity] = jnp.where(
            element == asked, 1.0, 0.0
        ).astype(BF16)
    element = lax.broadcasted_iota(jnp.int32, (width, receivers), 0)
    select_ref[:, slots * capacity : slots * capacity + receivers] = jnp.where(
        element == receiver_ref[...], 1.0, 0.0
    ).astype(BF16)
    values_ref = messages[-1]
    pack(field_ref[...], select_ref, weight_ref, messages[:-1], values_ref, rows // basis, basis)


def own_kernel_a(field_ref, matrix_ref, choose_ref, terms_ref, gathered_ref, rhs_ref):
    faces = choose_ref.shape[0]
    locals_, rows_all, width = terms_ref.shape
    basis = matrix_ref.shape[0] // (locals_ + faces)
    quantities = rows_all // basis
    clear_fill(rhs_ref, basis)

    def modal(q, carry):
        rows = pl.ds(pl.multiple_of(q * basis, 8), basis)
        stack_columns(field_ref[rows, :], rhs_ref)
        for at in range(0, width, 2 * LANES):
            lanes = slice(at, min(at + 2 * LANES, width))
            result = dot(matrix_ref[...], rhs_ref[:, lanes])
            for n in range(locals_):
                terms_ref[n, rows, lanes] = result[n * basis : (n + 1) * basis]
            for f in range(faces):
                n = locals_ + f
                gathered_ref[f, rows, lanes] = result[n * basis : (n + 1) * basis]
        return carry

    lax.fori_loop(0, quantities, modal, 0)

    def gather(f, carry):
        gathered_ref[f] = pick(gathered_ref[f], choose_ref[f])
        return carry

    lax.fori_loop(0, faces, gather, 0)


def own_kernel_b(field_ref, terms_ref, star_ref, local_ref, out_ref):
    quantities, _, stars, width = star_ref.shape
    basis = field_ref.shape[0] // quantities
    matrices = [(star_ref, n, 1, terms_ref, n) for n in range(stars)] + [
        (local_ref, f, -1, terms_ref, stars + f) for f in range(local_ref.shape[2])
    ]

    def tile_body(tile, carry):
        def base(p, lanes):
            return field_ref[p * basis : (p + 1) * basis, lanes]

        def emit(p, lanes, value):
            out_ref[p * basis : (p + 1) * basis, lanes] = value

        apply_maps(tile, matrices, base, emit, quantities, basis)
        return carry

    lax.fori_loop(0, width // LANES, tile_body, 0)


def halo_kernel(slots, sends, live_ref, field_ref, partial_ref, gathered_ref, matrix_ref, remote_ref, choose_ref, energy_ref, select_ref, weight_ref, *rest):
    halo_refs = rest[:slots]
    state_ref, power_ref, values_ref = rest[slots : slots + 3]
    messages = rest[slots + 3 : slots + 3 + sends]
    columns_ref, flux_ref, terms_ref, rhs_ref = rest[slots + 3 + sends :]
    quantities, _, faces = remote_ref.shape[:3]
    rows_all, width = field_ref.shape
    basis = rows_all // quantities
    clear_fill(rhs_ref, basis)
    lane = lax.broadcasted_iota(jnp.int32, (SEND_ROWS, LANES), 1) < HALF
    for pair in range(slots // 2):
        a = halo_refs[2 * pair][...]
        b = halo_refs[2 * pair + 1][...]
        lanes = slice(pair * LANES, (pair + 1) * LANES)
        columns_ref[0:SEND_ROWS, lanes] = jnp.where(lane, a, pltpu.roll(b, HALF, 1))
        bottom = jnp.where(lane, pltpu.roll(a, HALF, 1), b)
        columns_ref[SEND_ROWS:, lanes] = bottom[: rows_all - SEND_ROWS]

    def modal(q, carry):
        rows = pl.ds(pl.multiple_of(q * basis, 8), basis)
        stack_columns(columns_ref[rows, :], rhs_ref)
        result = dot(matrix_ref[...], rhs_ref[...])
        for f in range(faces):
            flux_ref[f, rows, :] = result[f * basis : (f + 1) * basis]
        return carry

    lax.fori_loop(0, quantities, modal, 0)

    def gather(f, carry):
        terms_ref[f] = gathered_ref[f] + pick(flux_ref[f], choose_ref[f])
        return carry

    lax.fori_loop(0, faces, gather, 0)
    matrices = [(remote_ref, f, -1, terms_ref, f) for f in range(faces)]

    def tile_body(tile, power):
        totals = [power]

        def base(p, lanes):
            return partial_ref[p * basis : (p + 1) * basis, lanes]

        def emit(p, lanes, value):
            live = live_ref[0:1, lanes] > 0
            kept = jnp.where(live, value, field_ref[p * basis : (p + 1) * basis, lanes])
            state_ref[p * basis : (p + 1) * basis, lanes] = kept
            squares = kept * kept * energy_ref[p : p + 1, lanes]
            for block in range(basis // 8):
                totals[0] = totals[0] + squares[block * 8 : (block + 1) * 8]

        apply_maps(tile, matrices, base, emit, quantities, basis)
        return totals[0]

    power_ref[...] = lax.fori_loop(0, width // LANES, tile_body, jnp.zeros((8, LANES), F32))
    pack(state_ref[...], select_ref, weight_ref, messages, values_ref, quantities, basis)


def vmem(count):
    return [pl.BlockSpec(memory_space=pltpu.VMEM)] * count


def smem(count):
    return [pl.BlockSpec(memory_space=pltpu.SMEM)] * count


def granted(mib, flops=0):
    extra = {}
    if flops:
        extra["cost_estimate"] = pl.CostEstimate(flops=flops, bytes_accessed=8_000_000, transcendentals=0)
    return dict(compiler_params=pltpu.CompilerParams(vmem_limit_bytes=mib * 2**20), **extra)


def per_device(
    element_state,
    stiffness,
    flux_local,
    flux_remote,
    star_matrix,
    face_local,
    face_remote,
    energy_weight,
    face_neighbour,
    element_count,
    send_count,
    send_element,
    receiver_element,
    receiver_slot,
    receiver_weight,
):
    basis, quantities, width = element_state.shape
    slots, capacity = send_element.shape[1:]
    faces = face_neighbour.shape[0]
    receivers = receiver_slot.shape[0]
    group_size = lax.axis_size("dom")
    rows = basis * quantities
    locals_ = stiffness.shape[0] + faces
    halo_width = slots * capacity

    fields = element_state.transpose(1, 0, 2).reshape(rows, width)
    star = star_matrix.transpose(1, 2, 0, 3)
    local = face_local.transpose(1, 2, 0, 3)
    remote = face_remote.transpose(1, 2, 0, 3)

    message = jax.ShapeDtypeStruct((SEND_ROWS, LANES), F32)
    values_shape = jax.ShapeDtypeStruct((quantities, receivers), F32)
    field_shape = jax.ShapeDtypeStruct((rows, width), F32)
    power_shape = jax.ShapeDtypeStruct((8, LANES), F32)
    terms_shape = jax.ShapeDtypeStruct((locals_, rows, width), F32)
    gathered_shape = jax.ShapeDtypeStruct((faces, rows, width), F32)
    select_shape = jax.ShapeDtypeStruct((width, halo_width + LANES), BF16)
    outs = pl.pallas_call(
        first_kernel,
        out_shape=(select_shape,) + (message,) * slots + (values_shape,),
        in_specs=smem(1) + vmem(4),
        out_specs=tuple(vmem(slots + 2)),
        name="first_messages",
        **granted(16),
    )(send_count, fields, send_element[0], receiver_element[None, :], receiver_weight)
    select, messages = outs[0], outs[1:-1]

    element_row = jnp.arange(width, dtype=jnp.int32)[:, None]
    choose_own = (element_row[None] == face_neighbour[:, None, :]).astype(BF16)
    halo_row = jnp.arange(halo_width, dtype=jnp.int32)[:, None] + width
    choose_halo = (halo_row[None] == face_neighbour[:, None, :]).astype(BF16)
    own_matrix = padded_k(jnp.concatenate([stiffness, flux_local, flux_remote], 0).reshape(-1, basis))
    halo_matrix = own_matrix[locals_ * basis :]

    live = (jnp.arange(width, dtype=jnp.int32) < element_count[0]).astype(F32)[None, :]
    live_energy = jnp.where(live > 0, energy_weight, 0.0)

    def send(slot, value):
        if slot < 2 * PEER_REACH:
            offset = slot + 1 if slot < PEER_REACH else PEER_REACH - 1 - slot
            pairs = [(i, (i + offset) % group_size) for i in range(group_size)]
            return lax.ppermute(value, "dom", pairs)
        offset = 1 if slot == 2 * PEER_REACH else -1
        count = lax.axis_size("grp")
        pairs = [(i, i + offset) for i in range(count) if 0 <= i + offset < count]
        return lax.ppermute(value, "grp", pairs)

    powers = []
    samples = []
    for step in range(TIME_STEPS):
        last = step == TIME_STEPS - 1
        arrived = [None] * slots
        for slot in FIRST_SENDS:
            arrived[slot] = send(slot, messages[slot])
        terms, gathered = pl.pallas_call(
            own_kernel_a,
            out_shape=(terms_shape, gathered_shape),
            in_specs=vmem(3),
            out_specs=tuple(vmem(2)),
            scratch_shapes=[pltpu.VMEM((3 * HALF, width), BF16)],
            name="own_terms_a",
            **granted(8, 5_000_000_000),
        )(fields, own_matrix, choose_own)
        others = [slot for slot in range(slots) if slot not in FIRST_SENDS]
        held = lax.optimization_barrier(tuple(messages[slot] for slot in others) + (gathered,))
        gathered = held[-1]
        for slot, value in zip(others, held):
            arrived[slot] = send(slot, value)
        partial = pl.pallas_call(
            own_kernel_b,
            out_shape=field_shape,
            in_specs=vmem(4),
            out_specs=vmem(1)[0],
            name="own_terms_b",
            **granted(4, 5_000_000_000),
        )(fields, terms, star, local)
        sends = 0 if last else slots
        outs = pl.pallas_call(
            lambda *refs, sends=sends: halo_kernel(slots, sends, *refs),
            out_shape=(field_shape, power_shape, values_shape) + (message,) * sends,
            in_specs=vmem(10 + slots),
            out_specs=tuple(vmem(3 + sends)),
            scratch_shapes=[
                pltpu.VMEM((rows, halo_width), F32),
                pltpu.VMEM((faces, rows, halo_width), F32),
                pltpu.VMEM((faces, rows, width), F32),
                pltpu.VMEM((3 * HALF, halo_width), BF16),
            ],
            name="halo_terms_last" if last else "halo_terms",
            **granted(18, 6_000_000_000),
        )(live, fields, partial, gathered, halo_matrix, remote, choose_halo, live_energy, select, receiver_weight, *arrived)
        fields, messages = outs[0], outs[3:]
        powers.append(outs[1])
        samples.append(outs[2])

    new_state = fields.reshape(quantities, basis, width).transpose(1, 0, 2)
    denominator = float(group_size * width * basis * quantities)
    own_energy = 0.5 * jnp.sum(jnp.stack(powers), axis=(1, 2))
    values = jnp.concatenate(samples, 0)
    matches = (receiver_slot[:, None] == jnp.arange(group_size * receivers)[None, :]).astype(F32)
    placed = jnp.dot(values, matches, precision=highest, preferred_element_type=F32)
    pieces = placed.reshape(-1, group_size, receivers).transpose(1, 0, 2).reshape(group_size, -1)
    fill = jnp.zeros((group_size, 16 - TIME_STEPS), F32)
    spread = jnp.broadcast_to(own_energy[None, :], (group_size, TIME_STEPS))
    pieces = jnp.concatenate([pieces, spread, fill], 1)
    arrived = lax.all_to_all(pieces, "dom", split_axis=0, concat_axis=0, tiled=True)
    total = arrived.sum(axis=0)
    traces = total[: TIME_STEPS * quantities * receivers].reshape(TIME_STEPS, quantities, receivers)
    energy = total[TIME_STEPS * quantities * receivers :][:TIME_STEPS] / denominator
    return (new_state, energy[None, :], traces)


def solution(mesh):
    return jax.shard_map(
        per_device,
        mesh=mesh,
        in_specs=(
            P(None, None, GRP_DOM),
            P(),
            P(),
            P(),
            P(None, None, None, GRP_DOM),
            P(None, None, None, GRP_DOM),
            P(None, None, None, GRP_DOM),
            P(None, GRP_DOM),
            P(None, GRP_DOM),
            P(GRP_DOM),
            P(GRP_DOM, None),
            P(GRP_DOM, None, None),
            P(GRP_DOM),
            P(GRP_DOM),
            P(None, GRP_DOM),
        ),
        out_specs=(P(None, None, GRP_DOM), P("grp", None), P(None, None, GRP_DOM)),
        check_vma=False,
    )
```

profile of v0, /device:TPU:16, one launch (start us, length us, event | category | flops | bytes accessed | tf_op | source)
XLA Modules:
  0.0 172.8 jit_solution(18349070548394230660)
XLA Ops:
  0.6 0.9 copy.28.weight_ref.refs_9_
  1.5 1.0 pad_maximum_fusion
  2.6 1.8 %fusion.choose_ref = bf16[4,640,640]{2,1,0:T(8,128)(2,1)S(1)} fusion(s32[4,640]{1,0:T(4,128)} %param.23), kind=kLoop, calls=%fused_computation.1 | loop fusion | flops 3276800 | bytes 3287040 | tf_op jit(solution)/shard_map/convert_element_type | solution.py:295
  4.4 0.2 add_convert_fusion.matrix_ref
  4.8 9.0 %own_terms_a.3 = (f32[7,504,640]{2,1,0:T(8,128)S(1)}, f32[4,504,640]{2,1,0:T(8,128)S(1)}) custom-call(f32[504,640]{1,0:T(8,128)S(1)} %bitcast.27, bf16[616,192]{1,0:T(8,128)(2,1)S(1)} %add_convert_fusion.matrix_ref, bf16[4,640,640]{2,1,0:T(8,128)(2,1)S(1)} %fusion.choose_ref), custom_call_target="tpu_custom_call" | custom-call | flops 5000000000 | bytes 8000000 | tf_op jit(solution)/shard_map/own_terms_a/pallas_call | solution.py:321
  13.8 2.8 %first_messages.1 = (bf16[640,640]{1,0:T(8,128)(2,1)S(1)}, f32[256,128]{1,0:T(8,128)S(1)}, f32[256,128]{1,0:T(8,128)S(1)}, f32[256,128]{1,0:T(8,128)S(1)}, f32[2...) custom-call(s32[1,8]{1,0:T(1,128)S(1)} %copy-done.2, ...), custom_call_target="tpu_custom_call" | custom-call | tf_op jit(solution)/shard_map/first_messages/pallas_call | solution.py:284
  16.7 2.8 %collective-permute-start.2 = (f32[256,128]{1,0:T(8,128)S(1)}, f32[256,128]{1,0:T(8,128)S(1)}, u32[]{:S(2)}, u32[]{:S(2)}) collective-permute-start(f32[256,128]{1,0:T(8,128)S(1)} %get-tuple-element.64), channel_id=1, source_target_pairs={{0,3},{1,4},{2,5},{3,6},{4,7},{5,8},{6,9},{7,10},{8,11},{9,12},{10... | collective-permute-start | bytes 393224 | tf_op jit(solution)/shard_map/ppermute | solution.py:308
  19.4 5.3 %collective-permute-start.3 = (f32[256,128]{1,0:T(8,128)S(1)}, f32[256,128]{1,0:T(8,128)S(1)}, u32[]{:S(2)}, u32[]{:S(2)}) collective-permute-start(f32[256,128]{1,0:T(8,128)S(1)} %get-tuple-element.65), channel_id=1, source_target_pairs={{0,31},{1,0},{2,1},{3,2},{4,3},{5,4},{6,5},{7,6},{8,7},{9,8},{10,9... | collective-permute-start | bytes 393224 | tf_op jit(solution)/shard_map/ppermute | solution.py:308
  24.7 0.8 collective-permute-start.4
  25.5 0.9 collective-permute-start
  26.4 1.8 %collective-permute-start.1 = (f32[256,128]{1,0:T(8,128)S(1)}, f32[256,128]{1,0:T(8,128)S(1)}, u32[]{:S(2)}, u32[]{:S(2)}) collective-permute-start(f32[256,128]{1,0:T(8,128)S(1)} %get-tuple-element.63), channel_id=1, source_target_pairs={{0,2},{1,3},{2,4},{3,5},{4,6},{5,7},{6,8},{7,9},{8,10},{9,11},{10,... | collective-permute-start | bytes 393224 | tf_op jit(solution)/shard_map/ppermute | solution.py:308
  28.3 6.3 %own_terms_b.3.refs_2_ = f32[504,640]{1,0:T(8,128)S(1)} custom-call(f32[504,640]{1,0:T(8,128)S(1)} %bitcast.29, f32[7,504,640]{2,1,0:T(8,128)S(1)} %get-tuple-element.55.terms_ref, f32[9,9,3,640]{3,2,1,0:T(4,128)S(1)} %bitcast.36, f32[9,9,4,640]{3,2,1,0:T(4,128)S(1)} %bitcast.39), custom_call_target="tpu_custom_call" | custom-call | flops 5000000000 | bytes 8000000 | tf_op jit(solution)/shard_map/own_terms_b/pallas_call | solution.py:335
  34.7 0.5 compare_convert_fusion.refs_6_
  35.9 3.6 %collective-permute-start.5 = (f32[256,128]{1,0:T(8,128)S(1)}, f32[256,128]{1,0:T(8,128)S(1)}, u32[]{:S(2)}, u32[]{:S(2)}) collective-permute-start(f32[256,128]{1,0:T(8,128)S(1)} %get-tuple-element.67), channel_id=1, source_target_pairs={{0,29},{1,30},{2,31},{3,0},{4,1},{5,2},{6,3},{7,4},{8,5},{9,6},{10... | collective-permute-start | bytes 393224 | tf_op jit(solution)/shard_map/ppermute | solution.py:308
  39.4 1.9 %collective-permute-start.6 = (f32[256,128]{1,0:T(8,128)S(1)}, f32[256,128]{1,0:T(8,128)S(1)}, u32[]{:S(2)}, u32[]{:S(2)}) collective-permute-start(f32[256,128]{1,0:T(8,128)S(1)} %get-tuple-element.68), channel_id=1, source_target_pairs={{0,32},{32,64},{64,96},{96,128},{128,160},{160,192},{192,224},{1,3... | collective-permute-start | bytes 393224 | tf_op jit(solution)/shard_map/ppermute | solution.py:312
  41.3 3.8 %collective-permute-start.7 = (f32[256,128]{1,0:T(8,128)S(1)}, f32[256,128]{1,0:T(8,128)S(1)}, u32[]{:S(2)}, u32[]{:S(2)}) collective-permute-start(f32[256,128]{1,0:T(8,128)S(1)} %get-tuple-element.69), channel_id=1, source_target_pairs={{32,0},{64,32},{96,64},{128,96},{160,128},{192,160},{224,192},{33,... | collective-permute-start | bytes 393224 | tf_op jit(solution)/shard_map/ppermute | solution.py:312
  45.3 0.4 collective-permute-done.6.refs_16_
  45.7 1.8 %collective-permute-done.7.refs_17_ = f32[256,128]{1,0:T(8,128)S(1)} collective-permute-done((f32[256,128]{1,0:T(8,128)S(1)}, f32[256,128]{1,0:T(8,128)S(1)}, u32[]{:S(2)}, u32[]{:S(2)}) %collective-permute-start.7) | collective-permute-done | bytes 131104 | tf_op jit(solution)/shard_map/ppermute | solution.py:312
  47.5 12.3 %halo_terms.2 = (f32[504,640]{1,0:T(8,128)S(1)}, f32[8,128]{1,0:T(8,128)S(1)}, f32[9,16]{1,0:T(8,128)S(1)}, f32[256,128]{1,0:T(8,128)S(1)}, f32[256,128]{1,0:T(8...) custom-call(f32[1,640]{1,0:T(1,128)S(1)} %compare_convert_fusion.1.r, ...), custom_call_target="tpu_custom_call" | custom-call | flops 6000000000 | bytes 8000000 | tf_op jit(solution)/shard_map/halo_terms/pallas_call | solution.py:344
  59.8 9.0 %own_terms_a.4 = (f32[7,504,640]{2,1,0:T(8,128)S(1)}, f32[4,504,640]{2,1,0:T(8,128)S(1)}) custom-call(f32[504,640]{1,0:T(8,128)S(1)} %get-tuple-element.70.field_ref.refs_1_, bf16[616,192]{1,0:T(8,128)(2,1)S(1)} %add_convert_fusion.matrix_ref, bf16[4,640,640]{2,1,0:T(8,128)(2,1)S(1)} %fusion.choose_ref), custom_call_target="tpu_custom_call" | custom-call | flops 5000000000 | bytes 8000000 | tf_op jit(solution)/shard_map/own_terms_a/pallas_call | solution.py:321
  68.9 5.4 %collective-permute-start.11 = (f32[256,128]{1,0:T(8,128)S(1)}, f32[256,128]{1,0:T(8,128)S(1)}, u32[]{:S(2)}, u32[]{:S(2)}) collective-permute-start(f32[256,128]{1,0:T(8,128)S(1)} %get-tuple-element.80), channel_id=1, source_target_pairs={{0,31},{1,0},{2,1},{3,2},{4,3},{5,4},{6,5},{7,6},{8,7},{9,8},{10,9... | collective-permute-start | bytes 393224 | tf_op jit(solution)/shard_map/ppermute | solution.py:308
  74.3 0.8 collective-permute-start.12
  75.1 2.6 %collective-permute-start.14 = (f32[256,128]{1,0:T(8,128)S(1)}, f32[256,128]{1,0:T(8,128)S(1)}, u32[]{:S(2)}, u32[]{:S(2)}) collective-permute-start(f32[256,128]{1,0:T(8,128)S(1)} %get-tuple-element.83), channel_id=1, source_target_pairs={{0,32},{32,64},{64,96},{96,128},{128,160},{160,192},{192,224},{1,3... | collective-permute-start | bytes 393224 | tf_op jit(solution)/shard_map/ppermute | solution.py:312
  77.7 0.3 collective-permute-done.10.refs_12_
  78.0 2.7 %collective-permute-start.15 = (f32[256,128]{1,0:T(8,128)S(1)}, f32[256,128]{1,0:T(8,128)S(1)}, u32[]{:S(2)}, u32[]{:S(2)}) collective-permute-start(f32[256,128]{1,0:T(8,128)S(1)} %get-tuple-element.84), channel_id=1, source_target_pairs={{32,0},{64,32},{96,64},{128,96},{160,128},{192,160},{224,192},{33,... | collective-permute-start | bytes 393224 | tf_op jit(solution)/shard_map/ppermute | solution.py:312
  80.7 2.1 %collective-permute-start.8 = (f32[256,128]{1,0:T(8,128)S(1)}, f32[256,128]{1,0:T(8,128)S(1)}, u32[]{:S(2)}, u32[]{:S(2)}) collective-permute-start(f32[256,128]{1,0:T(8,128)S(1)} %get-tuple-element.77), channel_id=1, source_target_pairs={{0,1},{1,2},{2,3},{3,4},{4,5},{5,6},{6,7},{7,8},{8,9},{9,10},{10,1... | collective-permute-start | bytes 393224 | tf_op jit(solution)/shard_map/ppermute | solution.py:308
  82.8 0.5 collective-permute-done.12.refs_14_
  83.3 2.2 %collective-permute-start.9 = (f32[256,128]{1,0:T(8,128)S(1)}, f32[256,128]{1,0:T(8,128)S(1)}, u32[]{:S(2)}, u32[]{:S(2)}) collective-permute-start(f32[256,128]{1,0:T(8,128)S(1)} %get-tuple-element.78), channel_id=1, source_target_pairs={{0,2},{1,3},{2,4},{3,5},{4,6},{5,7},{6,8},{7,9},{8,10},{9,11},{10,... | collective-permute-start | bytes 393224 | tf_op jit(solution)/shard_map/ppermute | solution.py:308
  85.5 6.3 %own_terms_b.4.refs_2_ = f32[504,640]{1,0:T(8,128)S(1)} custom-call(f32[504,640]{1,0:T(8,128)S(1)} %get-tuple-element.70.field_ref.refs_1_, f32[7,504,640]{2,1,0:T(8,128)S(1)} %get-tuple-element.71.terms_ref, f32[9,9,3,640]{3,2,1,0:T(4,128)S(1)} %bitcast.37, f32[9,9,4,640]{3,2,1,0:T(4,128)S(1)} %bitcast.40), custom_call_target="tpu_custom_call" | custom-call | flops 5000000000 | bytes 8000000 | tf_op jit(solution)/shard_map/own_terms_b/pallas_call | solution.py:335
  91.8 1.2 collective-permute-done.9.refs_11_
  93.1 12.3 %halo_terms.3 = (f32[504,640]{1,0:T(8,128)S(1)}, f32[8,128]{1,0:T(8,128)S(1)}, f32[9,16]{1,0:T(8,128)S(1)}, f32[256,128]{1,0:T(8,128)S(1)}, f32[256,128]{1,0:T(8...) custom-call(f32[1,640]{1,0:T(1,128)S(1)} %compare_convert_fusion.1.r, ...), custom_call_target="tpu_custom_call" | custom-call | flops 6000000000 | bytes 8000000 | tf_op jit(solution)/shard_map/halo_terms/pallas_call | solution.py:344
  105.4 9.0 %own_terms_a.5 = (f32[7,504,640]{2,1,0:T(8,128)S(1)}, f32[4,504,640]{2,1,0:T(8,128)S(1)}) custom-call(f32[504,640]{1,0:T(8,128)S(1)} %get-tuple-element.85.field_ref.refs_1_, bf16[616,192]{1,0:T(8,128)(2,1)S(1)} %add_convert_fusion.matrix_ref, bf16[4,640,640]{2,1,0:T(8,128)(2,1)S(1)} %fusion.choose_ref), custom_call_target="tpu_custom_call" | custom-call | flops 5000000000 | bytes 8000000 | tf_op jit(solution)/shard_map/own_terms_a/pallas_call | solution.py:321
  114.4 0.7 collective-permute-start.18
  115.1 3.2 %collective-permute-start.19 = (f32[256,128]{1,0:T(8,128)S(1)}, f32[256,128]{1,0:T(8,128)S(1)}, u32[]{:S(2)}, u32[]{:S(2)}) collective-permute-start(f32[256,128]{1,0:T(8,128)S(1)} %get-tuple-element.95), channel_id=1, source_target_pairs={{0,31},{1,0},{2,1},{3,2},{4,3},{5,4},{6,5},{7,6},{8,7},{9,8},{10,9... | collective-permute-start | bytes 393224 | tf_op jit(solution)/shard_map/ppermute | solution.py:308
  118.3 2.4 %collective-permute-start.20 = (f32[256,128]{1,0:T(8,128)S(1)}, f32[256,128]{1,0:T(8,128)S(1)}, u32[]{:S(2)}, u32[]{:S(2)}) collective-permute-start(f32[256,128]{1,0:T(8,128)S(1)} %get-tuple-element.96), channel_id=1, source_target_pairs={{0,30},{1,31},{2,0},{3,1},{4,2},{5,3},{6,4},{7,5},{8,6},{9,7},{10,... | collective-permute-start | bytes 393224 | tf_op jit(solution)/shard_map/ppermute | solution.py:308
  120.8 1.2 collective-permute-start.17
  122.0 1.2 collective-permute-done.18.refs_12_
  123.2 3.8 %collective-permute-start.21 = (f32[256,128]{1,0:T(8,128)S(1)}, f32[256,128]{1,0:T(8,128)S(1)}, u32[]{:S(2)}, u32[]{:S(2)}) collective-permute-start(f32[256,128]{1,0:T(8,128)S(1)} %get-tuple-element.97), channel_id=1, source_target_pairs={{0,29},{1,30},{2,31},{3,0},{4,1},{5,2},{6,3},{7,4},{8,5},{9,6},{10... | collective-permute-start | bytes 393224 | tf_op jit(solution)/shard_map/ppermute | solution.py:308
  127.0 1.9 %collective-permute-start.22 = (f32[256,128]{1,0:T(8,128)S(1)}, f32[256,128]{1,0:T(8,128)S(1)}, u32[]{:S(2)}, u32[]{:S(2)}) collective-permute-start(f32[256,128]{1,0:T(8,128)S(1)} %get-tuple-element.98), channel_id=1, source_target_pairs={{0,32},{32,64},{64,96},{96,128},{128,160},{160,192},{192,224},{1,3... | collective-permute-start | bytes 393224 | tf_op jit(solution)/shard_map/ppermute | solution.py:312
  128.9 3.6 %collective-permute-start.23 = (f32[256,128]{1,0:T(8,128)S(1)}, f32[256,128]{1,0:T(8,128)S(1)}, u32[]{:S(2)}, u32[]{:S(2)}) collective-permute-start(f32[256,128]{1,0:T(8,128)S(1)} %get-tuple-element.99), channel_id=1, source_target_pairs={{32,0},{64,32},{96,64},{128,96},{160,128},{192,160},{224,192},{33,... | collective-permute-start | bytes 393224 | tf_op jit(solution)/shard_map/ppermute | solution.py:312
  132.6 6.3 %own_terms_b.5.refs_2_ = f32[504,640]{1,0:T(8,128)S(1)} custom-call(f32[504,640]{1,0:T(8,128)S(1)} %get-tuple-element.85.field_ref.refs_1_, f32[7,504,640]{2,1,0:T(8,128)S(1)} %get-tuple-element.86.terms_ref, f32[9,9,3,640]{3,2,1,0:T(4,128)S(1)} %bitcast.38, f32[9,9,4,640]{3,2,1,0:T(4,128)S(1)} %bitcast.41), custom_call_target="tpu_custom_call" | custom-call | flops 5000000000 | bytes 8000000 | tf_op jit(solution)/shard_map/own_terms_b/pallas_call | solution.py:335
  139.0 12.0 %halo_terms_last.1 = (f32[504,640]{1,0:T(8,128)}, f32[8,128]{1,0:T(8,128)S(1)}, f32[9,16]{1,0:T(8,128)S(1)}) custom-call(f32[1,640]{1,0:T(1,128)S(1)} %compare_convert_fusion.1.refs_0_, f32[504,640]{1,0:T(8,128)S(1)} %get-tuple-element.85.field_ref.refs_1_, f32[504,640]{1,0:T(8,128)S(1)} %own_terms_b.5.refs_2_, ...), custom_call_target="tpu_custom_call" | custom-call | flops 6000000000 | bytes 8000000 | tf_op jit(solution)/shard_map/halo_terms_last/pallas_call | solution.py:344
  151.2 0.2 fusion.1
  151.4 0.2 reshape.54
  151.6 0.2 copy.32
  152.0 19.4 %all_to_all.9 = f32[32,1,448]{2,1,0:T(1,128)S(1)} all-to-all(f32[32,1,448]{2,1,0:T(1,128)S(1)} %all_to_all.6), channel_id=1, replica_groups=mesh['grp'=8,'dom'=32] {'dom'}, dimensions={0} | all-to-all | bytes 114688 | tf_op jit(solution)/shard_map/all_to_all | solution.py:372
  171.5 0.6 multiply_bitcast_fusion
  172.2 0.6 copy.34
  (57 shorter events, 0.9 us)
Async XLA Ops:
  0.6 4.1 %copy-start = (f32[56,9,640]{2,0,1:T(8,128)S(1)}, f32[56,9,640]{2,0,1:T(8,128)}, u32[]{:S(2)}) copy-start(f32[56,9,640]{2,0,1:T(8,128)} %param.15) | copy-start | bytes 3870724
  4.7 9.1 %copy-start.1 = (s32[1,8,64]{2,1,0:T(8,128)S(1)}, s32[1,8,64]{2,1,0:T(8,128)}, u32[]{:S(2)}) copy-start(s32[1,8,64]{2,1,0:T(8,128)} %param.26) | copy-start | bytes 6148
  4.7 9.1 %copy-start.2 = (s32[1,8]{1,0:T(1,128)S(1)}, s32[1,8]{1,0:T(1,128)}, u32[]{:S(2)}) copy-start(s32[1,8]{1,0:T(1,128)} %count_ref.1) | copy-start | bytes 100
  4.7 9.1 %copy-start.3 = (s32[16]{0:T(128)S(1)}, s32[16]{0:T(128)}, u32[]{:S(2)}) copy-start(s32[16]{0:T(128)} %param.27) | copy-start | bytes 196
  4.7 23.5 %copy-start.4 = (f32[3,9,9,640]{3,0,2,1:T(4,128)S(1)}, f32[3,9,9,640]{3,0,2,1:T(4,128)}, u32[]{:S(2)}) copy-start(f32[3,9,9,640]{3,0,2,1:T(4,128)} %param.19) | copy-start | bytes 1866244
  4.7 23.5 %copy-start.5 = (f32[4,9,9,640]{3,0,2,1:T(4,128)S(1)}, f32[4,9,9,640]{3,0,2,1:T(4,128)}, u32[]{:S(2)}) copy-start(f32[4,9,9,640]{3,0,2,1:T(4,128)} %param.20) | copy-start | bytes 2488324
  16.7 19.2 %collective-permute-start.2 = (f32[256,128]{1,0:T(8,128)S(1)}, f32[256,128]{1,0:T(8,128)S(1)}, u32[]{:S(2)}, u32[]{:S(2)}) collective-permute-start(f32[256,128]{1,0:T(8,128)S(1)} %get-tuple-element.64), channel_id=1, source_target_pairs={{0,3},{1,4},{2,5},{3,6},{4,7},{5,8},{6,9},{7,10},{8,11},{9,12},{10... | collective-permute-start | bytes 393224 | tf_op jit(solution)/shard_map/ppermute | solution.py:308
  19.4 20.0 %collective-permute-start.3 = (f32[256,128]{1,0:T(8,128)S(1)}, f32[256,128]{1,0:T(8,128)S(1)}, u32[]{:S(2)}, u32[]{:S(2)}) collective-permute-start(f32[256,128]{1,0:T(8,128)S(1)} %get-tuple-element.65), channel_id=1, source_target_pairs={{0,31},{1,0},{2,1},{3,2},{4,3},{5,4},{6,5},{7,6},{8,7},{9,8},{10,9... | collective-permute-start | bytes 393224 | tf_op jit(solution)/shard_map/ppermute | solution.py:308
  24.7 16.6 %collective-permute-start.4 = (f32[256,128]{1,0:T(8,128)S(1)}, f32[256,128]{1,0:T(8,128)S(1)}, u32[]{:S(2)}, u32[]{:S(2)}) collective-permute-start(f32[256,128]{1,0:T(8,128)S(1)} %get-tuple-element.66), channel_id=1, source_target_pairs={{0,30},{1,31},{2,0},{3,1},{4,2},{5,3},{6,4},{7,5},{8,6},{9,7},{10,... | collective-permute-start | bytes 393224 | tf_op jit(solution)/shard_map/ppermute | solution.py:308
  25.5 19.7 %collective-permute-start = (f32[256,128]{1,0:T(8,128)S(1)}, f32[256,128]{1,0:T(8,128)S(1)}, u32[]{:S(2)}, u32[]{:S(2)}) collective-permute-start(f32[256,128]{1,0:T(8,128)S(1)} %get-tuple-element.62), channel_id=1, source_target_pairs={{0,1},{1,2},{2,3},{3,4},{4,5},{5,6},{6,7},{7,8},{8,9},{9,10},{10,1... | collective-permute-start | bytes 393224 | tf_op jit(solution)/shard_map/ppermute | solution.py:308
  26.4 18.8 %collective-permute-start.1 = (f32[256,128]{1,0:T(8,128)S(1)}, f32[256,128]{1,0:T(8,128)S(1)}, u32[]{:S(2)}, u32[]{:S(2)}) collective-permute-start(f32[256,128]{1,0:T(8,128)S(1)} %get-tuple-element.63), channel_id=1, source_target_pairs={{0,2},{1,3},{2,4},{3,5},{4,6},{5,7},{6,8},{7,9},{8,10},{9,11},{10,... | collective-permute-start | bytes 393224 | tf_op jit(solution)/shard_map/ppermute | solution.py:308
  28.3 6.4 %copy-start.8 = (s32[4,640]{1,0:T(4,128)S(1)}, s32[4,640]{1,0:T(4,128)}, u32[]{:S(2)}) copy-start(s32[4,640]{1,0:T(4,128)} %param.23) | copy-start | bytes 30724
  28.3 16.9 %copy-start.7 = (f32[9,640]{1,0:T(8,128)S(1)}, f32[9,640]{1,0:T(8,128)}, u32[]{:S(2)}) copy-start(f32[9,640]{1,0:T(8,128)} %param.22) | copy-start | bytes 69124
  28.3 19.2 %copy-start.6 = (f32[4,9,9,640]{3,0,2,1:T(4,128)S(1)}, f32[4,9,9,640]{3,0,2,1:T(4,128)}, u32[]{:S(2)}) copy-start(f32[4,9,9,640]{3,0,2,1:T(4,128)} %param.21) | copy-start | bytes 2488324
  35.9 9.4 %collective-permute-start.5 = (f32[256,128]{1,0:T(8,128)S(1)}, f32[256,128]{1,0:T(8,128)S(1)}, u32[]{:S(2)}, u32[]{:S(2)}) collective-permute-start(f32[256,128]{1,0:T(8,128)S(1)} %get-tuple-element.67), channel_id=1, source_target_pairs={{0,29},{1,30},{2,31},{3,0},{4,1},{5,2},{6,3},{7,4},{8,5},{9,6},{10... | collective-permute-start | bytes 393224 | tf_op jit(solution)/shard_map/ppermute | solution.py:308
  39.4 6.3 %collective-permute-start.6 = (f32[256,128]{1,0:T(8,128)S(1)}, f32[256,128]{1,0:T(8,128)S(1)}, u32[]{:S(2)}, u32[]{:S(2)}) collective-permute-start(f32[256,128]{1,0:T(8,128)S(1)} %get-tuple-element.68), channel_id=1, source_target_pairs={{0,32},{32,64},{64,96},{96,128},{128,160},{160,192},{192,224},{1,3... | collective-permute-start | bytes 393224 | tf_op jit(solution)/shard_map/ppermute | solution.py:312
  41.3 6.1 %collective-permute-start.7 = (f32[256,128]{1,0:T(8,128)S(1)}, f32[256,128]{1,0:T(8,128)S(1)}, u32[]{:S(2)}, u32[]{:S(2)}) collective-permute-start(f32[256,128]{1,0:T(8,128)S(1)} %get-tuple-element.69), channel_id=1, source_target_pairs={{32,0},{64,32},{96,64},{128,96},{160,128},{192,160},{224,192},{33,... | collective-permute-start | bytes 393224 | tf_op jit(solution)/shard_map/ppermute | solution.py:312
  68.8 9.2 %collective-permute-start.10 = (f32[256,128]{1,0:T(8,128)S(1)}, f32[256,128]{1,0:T(8,128)S(1)}, u32[]{:S(2)}, u32[]{:S(2)}) collective-permute-start(f32[256,128]{1,0:T(8,128)S(1)} %get-tuple-element.79), channel_id=1, source_target_pairs={{0,3},{1,4},{2,5},{3,6},{4,7},{5,8},{6,9},{7,10},{8,11},{9,12},{10... | collective-permute-start | bytes 393224 | tf_op jit(solution)/shard_map/ppermute | solution.py:308
  68.9 11.8 %collective-permute-start.11 = (f32[256,128]{1,0:T(8,128)S(1)}, f32[256,128]{1,0:T(8,128)S(1)}, u32[]{:S(2)}, u32[]{:S(2)}) collective-permute-start(f32[256,128]{1,0:T(8,128)S(1)} %get-tuple-element.80), channel_id=1, source_target_pairs={{0,31},{1,0},{2,1},{3,2},{4,3},{5,4},{6,5},{7,6},{8,7},{9,8},{10,9... | collective-permute-start | bytes 393224 | tf_op jit(solution)/shard_map/ppermute | solution.py:308
  74.3 9.0 %collective-permute-start.12 = (f32[256,128]{1,0:T(8,128)S(1)}, f32[256,128]{1,0:T(8,128)S(1)}, u32[]{:S(2)}, u32[]{:S(2)}) collective-permute-start(f32[256,128]{1,0:T(8,128)S(1)} %get-tuple-element.81), channel_id=1, source_target_pairs={{0,30},{1,31},{2,0},{3,1},{4,2},{5,3},{6,4},{7,5},{8,6},{9,7},{10,... | collective-permute-start | bytes 393224 | tf_op jit(solution)/shard_map/ppermute | solution.py:308
  75.1 16.7 %collective-permute-start.13 = (f32[256,128]{1,0:T(8,128)S(1)}, f32[256,128]{1,0:T(8,128)S(1)}, u32[]{:S(2)}, u32[]{:S(2)}) collective-permute-start(f32[256,128]{1,0:T(8,128)S(1)} %get-tuple-element.82), channel_id=1, source_target_pairs={{0,29},{1,30},{2,31},{3,0},{4,1},{5,2},{6,3},{7,4},{8,5},{9,6},{10... | collective-permute-start | bytes 393224 | tf_op jit(solution)/shard_map/ppermute | solution.py:308
  75.1 16.7 %collective-permute-start.14 = (f32[256,128]{1,0:T(8,128)S(1)}, f32[256,128]{1,0:T(8,128)S(1)}, u32[]{:S(2)}, u32[]{:S(2)}) collective-permute-start(f32[256,128]{1,0:T(8,128)S(1)} %get-tuple-element.83), channel_id=1, source_target_pairs={{0,32},{32,64},{64,96},{96,128},{128,160},{160,192},{192,224},{1,3... | collective-permute-start | bytes 393224 | tf_op jit(solution)/shard_map/ppermute | solution.py:312
  78.0 13.8 %collective-permute-start.15 = (f32[256,128]{1,0:T(8,128)S(1)}, f32[256,128]{1,0:T(8,128)S(1)}, u32[]{:S(2)}, u32[]{:S(2)}) collective-permute-start(f32[256,128]{1,0:T(8,128)S(1)} %get-tuple-element.84), channel_id=1, source_target_pairs={{32,0},{64,32},{96,64},{128,96},{160,128},{192,160},{224,192},{33,... | collective-permute-start | bytes 393224 | tf_op jit(solution)/shard_map/ppermute | solution.py:312
  80.7 11.2 %collective-permute-start.8 = (f32[256,128]{1,0:T(8,128)S(1)}, f32[256,128]{1,0:T(8,128)S(1)}, u32[]{:S(2)}, u32[]{:S(2)}) collective-permute-start(f32[256,128]{1,0:T(8,128)S(1)} %get-tuple-element.77), channel_id=1, source_target_pairs={{0,1},{1,2},{2,3},{3,4},{4,5},{5,6},{6,7},{7,8},{8,9},{9,10},{10,1... | collective-permute-start | bytes 393224 | tf_op jit(solution)/shard_map/ppermute | solution.py:308
  83.3 9.8 %collective-permute-start.9 = (f32[256,128]{1,0:T(8,128)S(1)}, f32[256,128]{1,0:T(8,128)S(1)}, u32[]{:S(2)}, u32[]{:S(2)}) collective-permute-start(f32[256,128]{1,0:T(8,128)S(1)} %get-tuple-element.78), channel_id=1, source_target_pairs={{0,2},{1,3},{2,4},{3,5},{4,6},{5,7},{6,8},{7,9},{8,10},{9,11},{10,... | collective-permute-start | bytes 393224 | tf_op jit(solution)/shard_map/ppermute | solution.py:308
  114.4 8.8 %collective-permute-start.18 = (f32[256,128]{1,0:T(8,128)S(1)}, f32[256,128]{1,0:T(8,128)S(1)}, u32[]{:S(2)}, u32[]{:S(2)}) collective-permute-start(f32[256,128]{1,0:T(8,128)S(1)} %get-tuple-element.94), channel_id=1, source_target_pairs={{0,3},{1,4},{2,5},{3,6},{4,7},{5,8},{6,9},{7,10},{8,11},{9,12},{10... | collective-permute-start | bytes 393224 | tf_op jit(solution)/shard_map/ppermute | solution.py:308
  115.1 11.9 %collective-permute-start.19 = (f32[256,128]{1,0:T(8,128)S(1)}, f32[256,128]{1,0:T(8,128)S(1)}, u32[]{:S(2)}, u32[]{:S(2)}) collective-permute-start(f32[256,128]{1,0:T(8,128)S(1)} %get-tuple-element.95), channel_id=1, source_target_pairs={{0,31},{1,0},{2,1},{3,2},{4,3},{5,4},{6,5},{7,6},{8,7},{9,8},{10,9... | collective-permute-start | bytes 393224 | tf_op jit(solution)/shard_map/ppermute | solution.py:308
  118.3 10.6 %collective-permute-start.20 = (f32[256,128]{1,0:T(8,128)S(1)}, f32[256,128]{1,0:T(8,128)S(1)}, u32[]{:S(2)}, u32[]{:S(2)}) collective-permute-start(f32[256,128]{1,0:T(8,128)S(1)} %get-tuple-element.96), channel_id=1, source_target_pairs={{0,30},{1,31},{2,0},{3,1},{4,2},{5,3},{6,4},{7,5},{8,6},{9,7},{10,... | collective-permute-start | bytes 393224 | tf_op jit(solution)/shard_map/ppermute | solution.py:308
  120.8 18.2 %collective-permute-start.16 = (f32[256,128]{1,0:T(8,128)S(1)}, f32[256,128]{1,0:T(8,128)S(1)}, u32[]{:S(2)}, u32[]{:S(2)}) collective-permute-start(f32[256,128]{1,0:T(8,128)S(1)} %get-tuple-element.92), channel_id=1, source_target_pairs={{0,1},{1,2},{2,3},{3,4},{4,5},{5,6},{6,7},{7,8},{8,9},{9,10},{10,1... | collective-permute-start | bytes 393224 | tf_op jit(solution)/shard_map/ppermute | solution.py:308
  120.8 18.2 %collective-permute-start.17 = (f32[256,128]{1,0:T(8,128)S(1)}, f32[256,128]{1,0:T(8,128)S(1)}, u32[]{:S(2)}, u32[]{:S(2)}) collective-permute-start(f32[256,128]{1,0:T(8,128)S(1)} %get-tuple-element.93), channel_id=1, source_target_pairs={{0,2},{1,3},{2,4},{3,5},{4,6},{5,7},{6,8},{7,9},{8,10},{9,11},{10,... | collective-permute-start | bytes 393224 | tf_op jit(solution)/shard_map/ppermute | solution.py:308
  123.2 15.7 %collective-permute-start.21 = (f32[256,128]{1,0:T(8,128)S(1)}, f32[256,128]{1,0:T(8,128)S(1)}, u32[]{:S(2)}, u32[]{:S(2)}) collective-permute-start(f32[256,128]{1,0:T(8,128)S(1)} %get-tuple-element.97), channel_id=1, source_target_pairs={{0,29},{1,30},{2,31},{3,0},{4,1},{5,2},{6,3},{7,4},{8,5},{9,6},{10... | collective-permute-start | bytes 393224 | tf_op jit(solution)/shard_map/ppermute | solution.py:308
  127.0 12.0 %collective-permute-start.22 = (f32[256,128]{1,0:T(8,128)S(1)}, f32[256,128]{1,0:T(8,128)S(1)}, u32[]{:S(2)}, u32[]{:S(2)}) collective-permute-start(f32[256,128]{1,0:T(8,128)S(1)} %get-tuple-element.98), channel_id=1, source_target_pairs={{0,32},{32,64},{64,96},{96,128},{128,160},{160,192},{192,224},{1,3... | collective-permute-start | bytes 393224 | tf_op jit(solution)/shard_map/ppermute | solution.py:312
  128.9 10.1 %collective-permute-start.23 = (f32[256,128]{1,0:T(8,128)S(1)}, f32[256,128]{1,0:T(8,128)S(1)}, u32[]{:S(2)}, u32[]{:S(2)}) collective-permute-start(f32[256,128]{1,0:T(8,128)S(1)} %get-tuple-element.99), channel_id=1, source_target_pairs={{32,0},{64,32},{96,64},{128,96},{160,128},{192,160},{224,192},{33,... | collective-permute-start | bytes 393224 | tf_op jit(solution)/shard_map/ppermute | solution.py:312
  138.9 12.3 %copy-start.9 = (s32[16]{0:T(128)S(1)}, s32[16]{0:T(128)}, u32[]{:S(2)}) copy-start(s32[16]{0:T(128)} %param.28) | copy-start | bytes 196
where the time goes:
time: 173 us
  Pallas kernels  85.6 us (49%)
  starting transfers between devices  53.5 us (31%)
  blocking collectives  19.4 us (11%)
  waiting for transfers between devices  5.5 us (3%)
  other arithmetic  4.46 us (3%)
  local copies, waits for them, and re-layouts  2.29 us (1%)
  between operations  1.76 us (1%)
    ppermute x18, starting transfers between devices, send(): return lax.ppermute(value, 'dom', pairs)  37 us
    pallas_call x3, Pallas kernels, per_device(): pl.pallas_call(lambda *refs, sends=sends: halo_kernel(slots, sends, *refs...  36.6 us
    pallas_call x3, Pallas kernels, per_device(): pl.pallas_call(own_kernel_a, out_shape=(terms_shape, gathered_shape), in_...  27.1 us
    all_to_all x1, blocking collectives, per_device(): lax.all_to_all(pieces, 'dom', split_axis=0, concat_axis=0, tiled=True)  19.4 us
    pallas_call x3, Pallas kernels, per_device(): pl.pallas_call(own_kernel_b, out_shape=field_shape, in_specs=vmem(4), out...  19 us
    ppermute x6, starting transfers between devices, send(): return lax.ppermute(value, 'grp', pairs)  16.6 us
  transfers between devices with their start and end apart: 24, of which 6 were waited for; matrix products, arithmetic and copies ran while one was open for 0% of the time, Pallas kernels for 11%

commit v1 on v0

--- a/solution.py
+++ b/solution.py
@@ -53,12 +53,49 @@
         )
 
 
+def pick_parts(high, low, chosen):
+    width = high.shape[1]
+    body = width - LANES
+    ends = jnp.concatenate([high[:, body:], low[:, body:]], 1)
+    return dot(high[:, :body], chosen[:body]) + dot(low[:, :body], chosen[:body]) + dot(ends, chosen[body:])
+
+
 def pick(field, chosen):
     high, low = two_parts(field)
+    if chosen.shape[0] > field.shape[1]:
+        return pick_parts(high, low, chosen)
     return dot(high, chosen) + dot(low, chosen)
 
 
-def apply_maps(tile, matrices, base, emit, quantities, basis):
+def apply_maps(unit, matrices, base, emit, quantities, basis, unroll):
+    group = 3
+    tile, part = unit // group, unit % group
+    lanes = pl.ds(pl.multiple_of(tile * LANES, LANES), LANES)
+
+    def column(q, total):
+        total = list(total)
+        rows = pl.ds(pl.multiple_of(q * basis, 8), basis)
+        for ref, at, sign, terms_ref, slot in matrices:
+            term = terms_ref[slot, rows, lanes]
+            for k in range(group):
+                product = ref[group * part + k, q, at : at + 1, lanes] * term
+                total[k] = total[k] + product if sign > 0 else total[k] - product
+        return tuple(total)
+
+    def rows_of(k):
+        return pl.ds(pl.multiple_of((group * part + k) * basis, 8), basis)
+
+    total = tuple(base(rows_of(k), lanes) for k in range(group))
+    if unroll:
+        for q in range(quantities):
+            total = column(q, total)
+    else:
+        total = lax.fori_loop(0, quantities, column, total)
+    for k in range(group):
+        emit(rows_of(k), lanes, total[k])
+
+
+def apply_tile(tile, matrices, base, emit, quantities, basis):
     lanes = pl.ds(pl.multiple_of(tile * LANES, LANES), LANES)
     group = 3
     for first in range(0, quantities, group):
@@ -103,12 +140,14 @@
 
 
 def first_kernel(count_ref, field_ref, send_ref, receiver_ref, weight_ref, select_ref, *messages):
-    rows, width = field_ref.shape
+    rows = field_ref.shape[0]
+    width = select_ref.shape[0]
     basis = weight_ref.shape[0]
     slots, capacity = send_ref.shape
     receivers = receiver_ref.shape[1]
     select_ref[:, slots * capacity :] = jnp.zeros((width, LANES), BF16)
     element = lax.broadcasted_iota(jnp.int32, (width, capacity), 0)
+    element = jnp.where(element < field_ref.shape[1], element, element - LANES)
     place = lax.broadcasted_iota(jnp.int32, (1, capacity), 1)
     for slot in range(slots):
         asked = jnp.where(place < count_ref[0, slot], send_ref[slot : slot + 1, :], -1)
@@ -116,6 +155,7 @@
             element == asked, 1.0, 0.0
         ).astype(BF16)
     element = lax.broadcasted_iota(jnp.int32, (width, receivers), 0)
+    element = jnp.where(element < field_ref.shape[1], element, element - LANES)
     select_ref[:, slots * capacity : slots * capacity + receivers] = jnp.where(
         element == receiver_ref[...], 1.0, 0.0
     ).astype(BF16)
@@ -123,56 +163,85 @@
     pack(field_ref[...], select_ref, weight_ref, messages[:-1], values_ref, rows // basis, basis)
 
 
-def own_kernel_a(field_ref, matrix_ref, choose_ref, terms_ref, gathered_ref, rhs_ref):
-    faces = choose_ref.shape[0]
+def own_maps(star_ref, local_ref, terms_ref):
+    stars = star_ref.shape[2]
+    return [(star_ref, n, 1, terms_ref, n) for n in range(stars)] + [
+        (local_ref, f, -1, terms_ref, stars + f) for f in range(local_ref.shape[2])
+    ]
+
+
+def own_kernel_a(field_ref, matrix_ref, star_ref, local_ref, terms_ref, high_ref, low_ref, out_ref, rhs_ref, flux_ref):
+    faces = high_ref.shape[0]
     locals_, rows_all, width = terms_ref.shape
     basis = matrix_ref.shape[0] // (locals_ + faces)
     quantities = rows_all // basis
     clear_fill(rhs_ref, basis)
 
-    def modal(q, carry):
-        rows = pl.ds(pl.multiple_of(q * basis, 8), basis)
-        stack_columns(field_ref[rows, :], rhs_ref)
-        for at in range(0, width, 2 * LANES):
-            lanes = slice(at, min(at + 2 * LANES, width))
-            result = dot(matrix_ref[...], rhs_ref[:, lanes])
-            for n in range(locals_):
-                terms_ref[n, rows, lanes] = result[n * basis : (n + 1) * basis]
-            for f in range(faces):
-                n = locals_ + f
-                gathered_ref[f, rows, lanes] = result[n * basis : (n + 1) * basis]
-        return carry
-
-    lax.fori_loop(0, quantities, modal, 0)
-
-    def gather(f, carry):
-        gathered_ref[f] = pick(gathered_ref[f], choose_ref[f])
-        return carry
-
-    lax.fori_loop(0, faces, gather, 0)
-
-
-def own_kernel_b(field_ref, terms_ref, star_ref, local_ref, out_ref):
-    quantities, _, stars, width = star_ref.shape
+    def modal(first, count):
+        for k in range(count):
+            rows = pl.ds(pl.multiple_of((first + k) * basis, 8), basis)
+            stack_columns(field_ref[rows, :], rhs_ref.at[:, k * width : (k + 1) * width])
+        for at in range(0, count * width, 2 * LANES):
+            end = min(at + 2 * LANES, count * width)
+            result = dot(matrix_ref[...], rhs_ref[:, at:end])
+            for low in range(at, end, LANES):
+                k, lane = low // width, low % width
+                rows = pl.ds(pl.multiple_of((first + k) * basis, 8), basis)
+                for n in range(locals_ + faces):
+                    value = result[n * basis : (n + 1) * basis, low - at : low - at + LANES]
+                    if n < locals_:
+                        terms_ref[n, rows, lane : lane + LANES] = value
+                    else:
+                        flux_ref[n - locals_, rows, lane : lane + LANES] = value
+
+    def pair(i, carry):
+        modal(2 * i, 2)
+        return carry
+
+    lax.fori_loop(0, quantities // 2, pair, 0)
+    if quantities % 2:
+        modal(quantities - 1, 1)
+
+    def parts(f, carry):
+        high_ref[f], low_ref[f] = two_parts(flux_ref[f])
+        return carry
+
+    lax.fori_loop(0, faces, parts, 0)
+
+    def base(rows, lanes):
+        return field_ref[rows, lanes]
+
+    def emit(rows, lanes, value):
+        out_ref[rows, :] = value
+
+    def plain(unit, carry):
+        apply_maps(unit, own_maps(star_ref, local_ref, terms_ref), base, emit, quantities, basis, False)
+        return carry
+
+    units = 3 * width // LANES
+    lax.fori_loop(units - 3, units, plain, 0)
+
+
+def own_kernel_b(field_ref, terms_ref, star_ref, local_ref, high_ref, low_ref, choose_ref, out_ref, gathered_ref):
+    quantities = star_ref.shape[0]
     basis = field_ref.shape[0] // quantities
-    matrices = [(star_ref, n, 1, terms_ref, n) for n in range(stars)] + [
-        (local_ref, f, -1, terms_ref, stars + f) for f in range(local_ref.shape[2])
-    ]
-
-    def tile_body(tile, carry):
-        def base(p, lanes):
-            return field_ref[p * basis : (p + 1) * basis, lanes]
-
-        def emit(p, lanes, value):
-            out_ref[p * basis : (p + 1) * basis, lanes] = value
-
-        apply_maps(tile, matrices, base, emit, quantities, basis)
-        return carry
-
-    lax.fori_loop(0, width // LANES, tile_body, 0)
-
-
-def halo_kernel(slots, sends, live_ref, field_ref, partial_ref, gathered_ref, matrix_ref, remote_ref, choose_ref, energy_ref, select_ref, weight_ref, *rest):
+
+    def base(rows, lanes):
+        return field_ref[rows, lanes]
+
+    def emit(rows, lanes, value):
+        out_ref[rows, lanes] = value
+
+    def face(f, carry):
+        gathered_ref[f] = pick_parts(high_ref[f], low_ref[f], choose_ref[f])
+        for k in range(3):
+            apply_maps(3 * f + k, own_maps(star_ref, local_ref, terms_ref), base, emit, quantities, basis, True)
+        return carry
+
+    lax.fori_loop(0, high_ref.shape[0], face, 0)
+
+
+def halo_kernel(slots, sends, live_ref, field_ref, partial_ref, partial_b_ref, gathered_ref, matrix_ref, remote_ref, choose_ref, energy_ref, select_ref, weight_ref, *rest):
     halo_refs = rest[:slots]
     state_ref, power_ref, values_ref = rest[slots : slots + 3]
     messages = rest[slots + 3 : slots + 3 + sends]
@@ -207,11 +276,12 @@
     lax.fori_loop(0, faces, gather, 0)
     matrices = [(remote_ref, f, -1, terms_ref, f) for f in range(faces)]
 
-    def tile_body(tile, power):
+    def tile_body(partial_ref, first, tile, power):
         totals = [power]
+        own = pl.ds(pl.multiple_of((tile - first) * LANES, LANES), LANES)
 
         def base(p, lanes):
-            return partial_ref[p * basis : (p + 1) * basis, lanes]
+            return partial_ref[p * basis : (p + 1) * basis, own]
 
         def emit(p, lanes, value):
             live = live_ref[0:1, lanes] > 0
@@ -221,10 +291,13 @@
             for block in range(basis // 8):
                 totals[0] = totals[0] + squares[block * 8 : (block + 1) * 8]
 
-        apply_maps(tile, matrices, base, emit, quantities, basis)
+        apply_tile(tile, matrices, base, emit, quantities, basis)
         return totals[0]
 
-    power_ref[...] = lax.fori_loop(0, width // LANES, tile_body, jnp.zeros((8, LANES), F32))
+    tiles = width // LANES
+    power = jnp.zeros((8, LANES), F32)
+    power = lax.fori_loop(0, tiles - 1, lambda tile, power: tile_body(partial_ref, 0, tile, power), power)
+    power_ref[...] = tile_body(partial_b_ref, tiles - 1, tiles - 1, power)
     pack(state_ref[...], select_ref, weight_ref, messages, values_ref, quantities, basis)
 
 
@@ -279,8 +352,9 @@
     field_shape = jax.ShapeDtypeStruct((rows, width), F32)
     power_shape = jax.ShapeDtypeStruct((8, LANES), F32)
     terms_shape = jax.ShapeDtypeStruct((locals_, rows, width), F32)
+    parts_shape = jax.ShapeDtypeStruct((faces, rows, width), BF16)
     gathered_shape = jax.ShapeDtypeStruct((faces, rows, width), F32)
-    select_shape = jax.ShapeDtypeStruct((width, halo_width + LANES), BF16)
+    select_shape = jax.ShapeDtypeStruct((width + LANES, halo_width + LANES), BF16)
     outs = pl.pallas_call(
         first_kernel,
         out_shape=(select_shape,) + (message,) * slots + (values_shape,),
@@ -291,7 +365,8 @@
     )(send_count, fields, send_element[0], receiver_element[None, :], receiver_weight)
     select, messages = outs[0], outs[1:-1]
 
-    element_row = jnp.arange(width, dtype=jnp.int32)[:, None]
+    element_row = jnp.arange(width + LANES, dtype=jnp.int32)[:, None]
+    element_row = jnp.where(element_row < width, element_row, element_row - LANES)
     choose_own = (element_row[None] == face_neighbour[:, None, :]).astype(BF16)
     halo_row = jnp.arange(halo_width, dtype=jnp.int32)[:, None] + width
     choose_halo = (halo_row[None] == face_neighbour[:, None, :]).astype(BF16)
@@ -318,33 +393,33 @@
         arrived = [None] * slots
         for slot in FIRST_SENDS:
             arrived[slot] = send(slot, messages[slot])
-        terms, gathered = pl.pallas_call(
+        terms, high, low, partial_b = pl.pallas_call(
             own_kernel_a,
-            out_shape=(terms_shape, gathered_shape),
-            in_specs=vmem(3),
-            out_specs=tuple(vmem(2)),
-            scratch_shapes=[pltpu.VMEM((3 * HALF, width), BF16)],
+            out_shape=(terms_shape, parts_shape, parts_shape, jax.ShapeDtypeStruct((rows, LANES), F32)),
+            in_specs=vmem(4),
+            out_specs=tuple(vmem(4)),
+            scratch_shapes=[pltpu.VMEM((3 * HALF, 2 * width), BF16), pltpu.VMEM((faces, rows, width), F32)],
             name="own_terms_a",
-            **granted(8, 5_000_000_000),
-        )(fields, own_matrix, choose_own)
+            **granted(10, 5_000_000_000),
+        )(fields, own_matrix, star, local)
         others = [slot for slot in range(slots) if slot not in FIRST_SENDS]
-        held = lax.optimization_barrier(tuple(messages[slot] for slot in others) + (gathered,))
-        gathered = held[-1]
+        held = lax.optimization_barrier(tuple(messages[slot] for slot in others) + (partial_b,))
+        partial_b = held[-1]
         for slot, value in zip(others, held):
             arrived[slot] = send(slot, value)
-        partial = pl.pallas_call(
+        partial, gathered = pl.pallas_call(
             own_kernel_b,
-            out_shape=field_shape,
-            in_specs=vmem(4),
-            out_specs=vmem(1)[0],
+            out_shape=(jax.ShapeDtypeStruct((rows, width - LANES), F32), gathered_shape),
+            in_specs=vmem(7),
+            out_specs=tuple(vmem(2)),
             name="own_terms_b",
-            **granted(4, 5_000_000_000),
-        )(fields, terms, star, local)
+            **granted(6, 5_000_000_000),
+        )(fields, terms, star, local, high, low, choose_own)
         sends = 0 if last else slots
         outs = pl.pallas_call(
             lambda *refs, sends=sends: halo_kernel(slots, sends, *refs),
             out_shape=(field_shape, power_shape, values_shape) + (message,) * sends,
-            in_specs=vmem(10 + slots),
+            in_specs=vmem(11 + slots),
             out_specs=tuple(vmem(3 + sends)),
             scratch_shapes=[
                 pltpu.VMEM((rows, halo_width), F32),
@@ -354,7 +429,7 @@
             ],
             name="halo_terms_last" if last else "halo_terms",
             **granted(18, 6_000_000_000),
-        )(live, fields, partial, gathered, halo_matrix, remote, choose_halo, live_energy, select, receiver_weight, *arrived)
+        )(live, fields, partial, partial_b, gathered, halo_matrix, remote, choose_halo, live_energy, select, receiver_weight, *arrived)
         fields, messages = outs[0], outs[3:]
         powers.append(outs[1])
         samples.append(outs[2])

time: 173 us -> 170 us (0.983)
  Pallas kernels: 85.6 us -> 79.3 us
  waiting for transfers between devices: 5.5 us -> 9.09 us
  local copies, waits for them, and re-layouts: 2.29 us -> 5.79 us
  blocking collectives: 19.4 us -> 17.5 us
    pallas_call x6, Pallas kernels: 46.2 us -> 40 us  [the longest x3 25.6 us: per_device(): pl.pallas_call(own_kernel_b, out_shape=(jax.ShapeDtypeStruct((rows, width...]
    ppermute x18, waiting for transfers between devices: 3.26 us -> 6.84 us  [send(): return lax.ppermute(value, 'dom', pairs)]
    unnamed x22 -> x28, local copies, waits for them, and re-layouts: 1.55 us -> 5.05 us
    all_to_all x1, blocking collectives: 19.4 us -> 17.5 us  [per_device(): lax.all_to_all(pieces, 'dom', split_axis=0, concat_axis=0, tiled=True)]
  transfers between devices with their start and end apart: 24 -> 24, of which waited for: 6 -> 6; matrix products, arithmetic and copies ran while one was open for 0% -> 1% of each run, Pallas kernels for 11% -> 15%
where the time goes in v1:
time: 170 us; the launch traced here: 169 us
  Pallas kernels  79.3 us (47%)
  starting transfers between devices  52.1 us (31%)
  blocking collectives  17.5 us (10%)
  waiting for transfers between devices  9.09 us (5%)
  local copies, waits for them, and re-layouts  5.79 us (3%)
  other arithmetic  3.35 us (2%)
  between operations  1.77 us (1%)
    ppermute x18, starting transfers between devices, send(): return lax.ppermute(value, 'dom', pairs)  37.1 us
    pallas_call x3, Pallas kernels, per_device(): pl.pallas_call(lambda *refs, sends=sends: halo_kernel(slots, sends, *refs...  36.7 us
    pallas_call x3, Pallas kernels, per_device(): pl.pallas_call(own_kernel_b, out_shape=(jax.ShapeDtypeStruct((rows, width...  25.6 us
    all_to_all x1, blocking collectives, per_device(): lax.all_to_all(pieces, 'dom', split_axis=0, concat_axis=0, tiled=True)  17.5 us
    ppermute x6, starting transfers between devices, send(): return lax.ppermute(value, 'grp', pairs)  15 us
    pallas_call x3, Pallas kernels, per_device(): pl.pallas_call(own_kernel_a, out_shape=(terms_shape, parts_shape, parts_s...  14.4 us
    ppermute x18, waiting for transfers between devices, send(): return lax.ppermute(value, 'dom', pairs)  6.84 us
    unnamed x28, local copies, waits for them, and re-layouts  5.05 us
  transfers between devices with their start and end apart: 24, of which 6 were waited for; matrix products, arithmetic and copies ran while one was open for 1% of the time, Pallas kernels for 15%

profile of v1, /device:TPU:16, one launch (start us, length us, event | category | flops | bytes accessed | tf_op | source)
XLA Modules:
  0.0 169.1 jit_solution(14216903530027752562)
XLA Ops:
  0.6 1.0 pad_maximum_fusion
  1.7 0.8 copy.28.weight_ref.refs_10_
  2.5 0.2 add_convert_fusion.matrix_ref
  2.8 1.1 copy-done
  3.9 1.1 copy-done.2
  5.0 1.3 copy-done.4
  6.4 4.8 %own_terms_a.3 = (f32[7,504,640]{2,1,0:T(8,128)S(1)}, bf16[4,504,640]{2,1,0:T(8,128)(2,1)S(1)}, bf16[4,504,640]{2,1,0:T(8,128)(2,1)S(1)}, f32[504,128]{1,0:T(8,128)S(1)}) custom-call(f32[504,640]{1,0:T(8,128)S(1)} %bitcast.39, bf16[616,192]{1,0:T(8,128)(2,1)S(1)} %add_convert_fusion.matrix_ref, f32[9,9,3,640]{3,2,1,0:T(4,128)S(1)} %bitcast.27, ...), custom_call_target="tpu_custom_call" | custom-call | flops 5000000000 | bytes 8000000 | tf_op jit(solution)/shard_map/own_terms_a/pallas_call | solution.py:396
  11.3 2.6 %first_messages.1 = (bf16[768,640]{1,0:T(8,128)(2,1)S(1)}, f32[256,128]{1,0:T(8,128)S(1)}, f32[256,128]{1,0:T(8,128)S(1)}, f32[256,128]{1,0:T(8,128)S(1)}, f32[2...) custom-call(s32[1,8]{1,0:T(1,128)S(1)} %copy-done.7, ...), custom_call_target="tpu_custom_call" | custom-call | tf_op jit(solution)/shard_map/first_messages/pallas_call | solution.py:358
  13.8 2.8 %collective-permute-start.2 = (f32[256,128]{1,0:T(8,128)S(1)}, f32[256,128]{1,0:T(8,128)S(1)}, u32[]{:S(2)}, u32[]{:S(2)}) collective-permute-start(f32[256,128]{1,0:T(8,128)S(1)} %get-tuple-element.80), channel_id=1, source_target_pairs={{0,3},{1,4},{2,5},{3,6},{4,7},{5,8},{6,9},{7,10},{8,11},{9,12},{10... | collective-permute-start | bytes 393224 | tf_op jit(solution)/shard_map/ppermute | solution.py:383
  16.6 5.3 %collective-permute-start.3 = (f32[256,128]{1,0:T(8,128)S(1)}, f32[256,128]{1,0:T(8,128)S(1)}, u32[]{:S(2)}, u32[]{:S(2)}) collective-permute-start(f32[256,128]{1,0:T(8,128)S(1)} %get-tuple-element.81), channel_id=1, source_target_pairs={{0,31},{1,0},{2,1},{3,2},{4,3},{5,4},{6,5},{7,6},{8,7},{9,8},{10,9... | collective-permute-start | bytes 393224 | tf_op jit(solution)/shard_map/ppermute | solution.py:383
  21.9 0.8 collective-permute-start.4
  22.7 0.9 collective-permute-start
  23.6 1.8 %collective-permute-start.1 = (f32[256,128]{1,0:T(8,128)S(1)}, f32[256,128]{1,0:T(8,128)S(1)}, u32[]{:S(2)}, u32[]{:S(2)}) collective-permute-start(f32[256,128]{1,0:T(8,128)S(1)} %get-tuple-element.79), channel_id=1, source_target_pairs={{0,2},{1,3},{2,4},{3,5},{4,6},{5,7},{6,8},{7,9},{8,10},{9,11},{10,... | collective-permute-start | bytes 393224 | tf_op jit(solution)/shard_map/ppermute | solution.py:383
  25.4 0.7 compare_convert_fusion.choose_ref
  26.2 8.5 %own_terms_b.3 = (f32[504,512]{1,0:T(8,128)S(1)}, f32[4,504,640]{2,1,0:T(8,128)S(1)}) custom-call(f32[504,640]{1,0:T(8,128)S(1)} %bitcast.41, f32[7,504,640]{2,1,0:T(8,128)S(1)} %get-tuple-element.67.terms_ref, f32[9,9,3,640]{3,2,1,0:T(4,128)S(1)} %bitcast.28, f32[9,9,4,640]{3,2,1,0:T(4,128)S(1)} %bitcast.34, ...), custom_call_target="tpu_custom_call" | custom-call | flops 5000000000 | bytes 8000000 | tf_op jit(solution)/shard_map/own_terms_b/pallas_call | solution.py:410
  34.7 0.5 compare_convert_fusion.1.refs_7_
  35.9 3.6 %collective-permute-start.5 = (f32[256,128]{1,0:T(8,128)S(1)}, f32[256,128]{1,0:T(8,128)S(1)}, u32[]{:S(2)}, u32[]{:S(2)}) collective-permute-start(f32[256,128]{1,0:T(8,128)S(1)} %get-tuple-element.83), channel_id=1, source_target_pairs={{0,29},{1,30},{2,31},{3,0},{4,1},{5,2},{6,3},{7,4},{8,5},{9,6},{10... | collective-permute-start | bytes 393224 | tf_op jit(solution)/shard_map/ppermute | solution.py:383
  39.5 1.9 %collective-permute-start.6 = (f32[256,128]{1,0:T(8,128)S(1)}, f32[256,128]{1,0:T(8,128)S(1)}, u32[]{:S(2)}, u32[]{:S(2)}) collective-permute-start(f32[256,128]{1,0:T(8,128)S(1)} %get-tuple-element.84), channel_id=1, source_target_pairs={{0,32},{32,64},{64,96},{96,128},{128,160},{160,192},{192,224},{1,3... | collective-permute-start | bytes 393224 | tf_op jit(solution)/shard_map/ppermute | solution.py:387
  41.4 3.8 %collective-permute-start.7 = (f32[256,128]{1,0:T(8,128)S(1)}, f32[256,128]{1,0:T(8,128)S(1)}, u32[]{:S(2)}, u32[]{:S(2)}) collective-permute-start(f32[256,128]{1,0:T(8,128)S(1)} %get-tuple-element.85), channel_id=1, source_target_pairs={{32,0},{64,32},{96,64},{128,96},{160,128},{192,160},{224,192},{33,... | collective-permute-start | bytes 393224 | tf_op jit(solution)/shard_map/ppermute | solution.py:387
  45.3 0.4 collective-permute-done.6.refs_17_
  45.8 1.8 %collective-permute-done.7.refs_18_ = f32[256,128]{1,0:T(8,128)S(1)} collective-permute-done((f32[256,128]{1,0:T(8,128)S(1)}, f32[256,128]{1,0:T(8,128)S(1)}, u32[]{:S(2)}, u32[]{:S(2)}) %collective-permute-start.7) | collective-permute-done | bytes 131104 | tf_op jit(solution)/shard_map/ppermute | solution.py:387
  47.6 12.2 %halo_terms.2 = (f32[504,640]{1,0:T(8,128)S(1)}, f32[8,128]{1,0:T(8,128)S(1)}, f32[9,16]{1,0:T(8,128)S(1)}, f32[256,128]{1,0:T(8,128)S(1)}, f32[256,128]{1,0:T(8...) custom-call(f32[1,640]{1,0:T(1,128)S(1)} %compare_convert_fusion.2.r, ...), custom_call_target="tpu_custom_call" | custom-call | flops 6000000000 | bytes 8000000 | tf_op jit(solution)/shard_map/halo_terms/pallas_call | solution.py:419
  59.8 4.8 %own_terms_a.4 = (f32[7,504,640]{2,1,0:T(8,128)S(1)}, bf16[4,504,640]{2,1,0:T(8,128)(2,1)S(1)}, bf16[4,504,640]{2,1,0:T(8,128)(2,1)S(1)}, f32[504,128]{1,0:T(8,128)S(1)}) custom-call(f32[504,640]{1,0:T(8,128)S(1)} %get-tuple-element.86.field_ref.refs_1_, bf16[616,192]{1,0:T(8,128)(2,1)S(1)} %add_convert_fusion.matrix_ref, f32[9,9,3,640]{3,2,1,0:T(4,128)S(1)} %bitcast.29, ...), custom_call_target="tpu_custom_call" | custom-call | flops 5000000000 | bytes 8000000 | tf_op jit(solution)/shard_map/own_terms_a/pallas_call | solution.py:396
  64.7 5.4 %collective-permute-start.11 = (f32[256,128]{1,0:T(8,128)S(1)}, f32[256,128]{1,0:T(8,128)S(1)}, u32[]{:S(2)}, u32[]{:S(2)}) collective-permute-start(f32[256,128]{1,0:T(8,128)S(1)} %get-tuple-element.100), channel_id=1, source_target_pairs={{0,31},{1,0},{2,1},{3,2},{4,3},{5,4},{6,5},{7,6},{8,7},{9,8},{10,9... | collective-permute-start | bytes 393224 | tf_op jit(solution)/shard_map/ppermute | solution.py:383
  70.1 0.8 collective-permute-start.12
  70.9 2.6 %collective-permute-start.14 = (f32[256,128]{1,0:T(8,128)S(1)}, f32[256,128]{1,0:T(8,128)S(1)}, u32[]{:S(2)}, u32[]{:S(2)}) collective-permute-start(f32[256,128]{1,0:T(8,128)S(1)} %get-tuple-element.103), channel_id=1, source_target_pairs={{0,32},{32,64},{64,96},{96,128},{128,160},{160,192},{192,224},{1,3... | collective-permute-start | bytes 393224 | tf_op jit(solution)/shard_map/ppermute | solution.py:387
  73.5 0.4 collective-permute-done.10.refs_13_
  73.8 2.6 %collective-permute-start.15 = (f32[256,128]{1,0:T(8,128)S(1)}, f32[256,128]{1,0:T(8,128)S(1)}, u32[]{:S(2)}, u32[]{:S(2)}) collective-permute-start(f32[256,128]{1,0:T(8,128)S(1)} %get-tuple-element.104), channel_id=1, source_target_pairs={{32,0},{64,32},{96,64},{128,96},{160,128},{192,160},{224,192},{33,... | collective-permute-start | bytes 393224 | tf_op jit(solution)/shard_map/ppermute | solution.py:387
  76.5 2.0 %collective-permute-start.8 = (f32[256,128]{1,0:T(8,128)S(1)}, f32[256,128]{1,0:T(8,128)S(1)}, u32[]{:S(2)}, u32[]{:S(2)}) collective-permute-start(f32[256,128]{1,0:T(8,128)S(1)} %get-tuple-element.97), channel_id=1, source_target_pairs={{0,1},{1,2},{2,3},{3,4},{4,5},{5,6},{6,7},{7,8},{8,9},{9,10},{10,1... | collective-permute-start | bytes 393224 | tf_op jit(solution)/shard_map/ppermute | solution.py:383
  78.5 0.6 collective-permute-done.12.refs_15_
  79.1 2.2 %collective-permute-start.9 = (f32[256,128]{1,0:T(8,128)S(1)}, f32[256,128]{1,0:T(8,128)S(1)}, u32[]{:S(2)}, u32[]{:S(2)}) collective-permute-start(f32[256,128]{1,0:T(8,128)S(1)} %get-tuple-element.98), channel_id=1, source_target_pairs={{0,2},{1,3},{2,4},{3,5},{4,6},{5,7},{6,8},{7,9},{8,10},{9,11},{10,... | collective-permute-start | bytes 393224 | tf_op jit(solution)/shard_map/ppermute | solution.py:383
  81.2 8.5 %own_terms_b.4 = (f32[504,512]{1,0:T(8,128)S(1)}, f32[4,504,640]{2,1,0:T(8,128)S(1)}) custom-call(f32[504,640]{1,0:T(8,128)S(1)} %get-tuple-element.86.field_ref.refs_1_, f32[7,504,640]{2,1,0:T(8,128)S(1)} %get-tuple-element.87.terms_ref, f32[9,9,3,640]{3,2,1,0:T(4,128)S(1)} %bitcast.30, f32[9,9,4,640]{3,2,1,0:T(4,128)S(1)} %bitcast.36, ...), custom_call_target="tpu_custom_call" | custom-call | flops 5000000000 | bytes 8000000 | tf_op jit(solution)/shard_map/own_terms_b/pallas_call | solution.py:410
  89.8 12.2 %halo_terms.3 = (f32[504,640]{1,0:T(8,128)S(1)}, f32[8,128]{1,0:T(8,128)S(1)}, f32[9,16]{1,0:T(8,128)S(1)}, f32[256,128]{1,0:T(8,128)S(1)}, f32[256,128]{1,0:T(8...) custom-call(f32[1,640]{1,0:T(1,128)S(1)} %compare_convert_fusion.2.r, ...), custom_call_target="tpu_custom_call" | custom-call | flops 6000000000 | bytes 8000000 | tf_op jit(solution)/shard_map/halo_terms/pallas_call | solution.py:419
  102.0 4.8 %own_terms_a.5 = (f32[7,504,640]{2,1,0:T(8,128)S(1)}, bf16[4,504,640]{2,1,0:T(8,128)(2,1)S(1)}, bf16[4,504,640]{2,1,0:T(8,128)(2,1)S(1)}, f32[504,128]{1,0:T(8,128)S(1)}) custom-call(f32[504,640]{1,0:T(8,128)S(1)} %get-tuple-element.105.field_ref.refs_1_, bf16[616,192]{1,0:T(8,128)(2,1)S(1)} %add_convert_fusion.matrix_ref, f32[9,9,3,640]{3,2,1,0:T(4,128)S(1)} %bitcast.31, ...), custom_call_target="tpu_custom_call" | custom-call | flops 5000000000 | bytes 8000000 | tf_op jit(solution)/shard_map/own_terms_a/pallas_call | solution.py:396
  106.9 1.9 %collective-permute-start.18 = (f32[256,128]{1,0:T(8,128)S(1)}, f32[256,128]{1,0:T(8,128)S(1)}, u32[]{:S(2)}, u32[]{:S(2)}) collective-permute-start(f32[256,128]{1,0:T(8,128)S(1)} %get-tuple-element.118), channel_id=1, source_target_pairs={{0,3},{1,4},{2,5},{3,6},{4,7},{5,8},{6,9},{7,10},{8,11},{9,12},{10... | collective-permute-start | bytes 393224 | tf_op jit(solution)/shard_map/ppermute | solution.py:383
  108.8 3.2 %collective-permute-start.19 = (f32[256,128]{1,0:T(8,128)S(1)}, f32[256,128]{1,0:T(8,128)S(1)}, u32[]{:S(2)}, u32[]{:S(2)}) collective-permute-start(f32[256,128]{1,0:T(8,128)S(1)} %get-tuple-element.119), channel_id=1, source_target_pairs={{0,31},{1,0},{2,1},{3,2},{4,3},{5,4},{6,5},{7,6},{8,7},{9,8},{10,9... | collective-permute-start | bytes 393224 | tf_op jit(solution)/shard_map/ppermute | solution.py:383
  112.0 1.1 collective-permute-start.20
  113.3 2.5 %collective-permute-start.17 = (f32[256,128]{1,0:T(8,128)S(1)}, f32[256,128]{1,0:T(8,128)S(1)}, u32[]{:S(2)}, u32[]{:S(2)}) collective-permute-start(f32[256,128]{1,0:T(8,128)S(1)} %get-tuple-element.117), channel_id=1, source_target_pairs={{0,2},{1,3},{2,4},{3,5},{4,6},{5,7},{6,8},{7,9},{8,10},{9,11},{10,... | collective-permute-start | bytes 393224 | tf_op jit(solution)/shard_map/ppermute | solution.py:383
  115.7 1.0 collective-permute-done.18.refs_13_
  116.7 2.7 %collective-permute-start.21 = (f32[256,128]{1,0:T(8,128)S(1)}, f32[256,128]{1,0:T(8,128)S(1)}, u32[]{:S(2)}, u32[]{:S(2)}) collective-permute-start(f32[256,128]{1,0:T(8,128)S(1)} %get-tuple-element.121), channel_id=1, source_target_pairs={{0,29},{1,30},{2,31},{3,0},{4,1},{5,2},{6,3},{7,4},{8,5},{9,6},{10... | collective-permute-start | bytes 393224 | tf_op jit(solution)/shard_map/ppermute | solution.py:383
  119.4 1.9 %collective-permute-start.22 = (f32[256,128]{1,0:T(8,128)S(1)}, f32[256,128]{1,0:T(8,128)S(1)}, u32[]{:S(2)}, u32[]{:S(2)}) collective-permute-start(f32[256,128]{1,0:T(8,128)S(1)} %get-tuple-element.122), channel_id=1, source_target_pairs={{0,32},{32,64},{64,96},{96,128},{128,160},{160,192},{192,224},{1,3... | collective-permute-start | bytes 393224 | tf_op jit(solution)/shard_map/ppermute | solution.py:387
  121.4 4.9 %collective-permute-done.20.refs_15_ = f32[256,128]{1,0:T(8,128)S(1)} collective-permute-done((f32[256,128]{1,0:T(8,128)S(1)}, f32[256,128]{1,0:T(8,128)S(1)}, u32[]{:S(2)}, u32[]{:S(2)}) %collective-permute-start.20) | collective-permute-done | bytes 131104 | tf_op jit(solution)/shard_map/ppermute | solution.py:383
  126.2 2.2 %collective-permute-start.23 = (f32[256,128]{1,0:T(8,128)S(1)}, f32[256,128]{1,0:T(8,128)S(1)}, u32[]{:S(2)}, u32[]{:S(2)}) collective-permute-start(f32[256,128]{1,0:T(8,128)S(1)} %get-tuple-element.123), channel_id=1, source_target_pairs={{32,0},{64,32},{96,64},{128,96},{160,128},{192,160},{224,192},{33,... | collective-permute-start | bytes 393224 | tf_op jit(solution)/shard_map/ppermute | solution.py:387
  128.4 8.5 %own_terms_b.5 = (f32[504,512]{1,0:T(8,128)S(1)}, f32[4,504,640]{2,1,0:T(8,128)S(1)}) custom-call(f32[504,640]{1,0:T(8,128)S(1)} %get-tuple-element.105.field_ref.refs_1_, f32[7,504,640]{2,1,0:T(8,128)S(1)} %get-tuple-element.106.terms_ref, f32[9,9,3,640]{3,2,1,0:T(4,128)S(1)} %bitcast.32, f32[9,9,4,640]{3,2,1,0:T(4,128)S(1)} %bitcast.38, ...), custom_call_target="tpu_custom_call" | custom-call | flops 5000000000 | bytes 8000000 | tf_op jit(solution)/shard_map/own_terms_b/pallas_call | solution.py:410
  137.0 12.3 %halo_terms_last.1 = (f32[504,640]{1,0:T(8,128)}, f32[8,128]{1,0:T(8,128)S(1)}, f32[9,16]{1,0:T(8,128)S(1)}) custom-call(f32[1,640]{1,0:T(1,128)S(1)} %compare_convert_fusion.2.refs_0_, f32[504,640]{1,0:T(8,128)S(1)} %get-tuple-element.105.field_ref.refs_1_, f32[504,512]{1,0:T(8,128)S(1)} %get-tuple-element.109.refs_2_, ...), custom_call_target="tpu_custom_call" | custom-call | flops 6000000000 | bytes 8000000 | tf_op jit(solution)/shard_map/halo_terms_last/pallas_call | solution.py:419
  150.3 17.5 %all_to_all.9 = f32[32,1,448]{2,1,0:T(1,128)S(1)} all-to-all(f32[32,1,448]{2,1,0:T(1,128)S(1)} %all_to_all.6), channel_id=1, replica_groups=mesh['grp'=8,'dom'=32] {'dom'}, dimensions={0} | all-to-all | bytes 114688 | tf_op jit(solution)/shard_map/all_to_all | solution.py:447
  167.8 0.6 multiply_bitcast_fusion
  168.5 0.6 copy.34
  (64 shorter events, 1.4 us)
Async XLA Ops:
  2.7 1.2 copy-start
  3.9 1.1 copy-start.2
  5.0 1.3 copy-start.4
  6.3 4.8 %copy-start.5 = (f32[56,9,640]{2,0,1:T(8,128)S(1)}, f32[56,9,640]{2,0,1:T(8,128)}, u32[]{:S(2)}) copy-start(f32[56,9,640]{2,0,1:T(8,128)} %param.15) | copy-start | bytes 3870724
  6.3 4.8 %copy-start.6 = (s32[1,8,64]{2,1,0:T(8,128)S(1)}, s32[1,8,64]{2,1,0:T(8,128)}, u32[]{:S(2)}) copy-start(s32[1,8,64]{2,1,0:T(8,128)} %param.26) | copy-start | bytes 6148
  6.4 4.9 %copy-start.7 = (s32[1,8]{1,0:T(1,128)S(1)}, s32[1,8]{1,0:T(1,128)}, u32[]{:S(2)}) copy-start(s32[1,8]{1,0:T(1,128)} %count_ref.1) | copy-start | bytes 100
  6.4 4.9 %copy-start.8 = (s32[16]{0:T(128)S(1)}, s32[16]{0:T(128)}, u32[]{:S(2)}) copy-start(s32[16]{0:T(128)} %param.27) | copy-start | bytes 196
  6.4 19.1 %copy-start.10 = (s32[4,640]{1,0:T(4,128)S(1)}, s32[4,640]{1,0:T(4,128)}, u32[]{:S(2)}) copy-start(s32[4,640]{1,0:T(4,128)} %param.23) | copy-start | bytes 30724
  11.2 14.9 %copy-start.1 = (f32[3,9,9,640]{3,0,2,1:T(4,128)S(1)}, f32[3,9,9,640]{3,0,2,1:T(4,128)}, u32[]{:S(2)}) copy-start(f32[3,9,9,640]{3,0,2,1:T(4,128)} %param.19) | copy-start | bytes 1866244
  11.2 14.9 %copy-start.3 = (f32[4,9,9,640]{3,0,2,1:T(4,128)S(1)}, f32[4,9,9,640]{3,0,2,1:T(4,128)}, u32[]{:S(2)}) copy-start(f32[4,9,9,640]{3,0,2,1:T(4,128)} %param.20) | copy-start | bytes 2488324
  13.8 22.1 %collective-permute-start.2 = (f32[256,128]{1,0:T(8,128)S(1)}, f32[256,128]{1,0:T(8,128)S(1)}, u32[]{:S(2)}, u32[]{:S(2)}) collective-permute-start(f32[256,128]{1,0:T(8,128)S(1)} %get-tuple-element.80), channel_id=1, source_target_pairs={{0,3},{1,4},{2,5},{3,6},{4,7},{5,8},{6,9},{7,10},{8,11},{9,12},{10... | collective-permute-start | bytes 393224 | tf_op jit(solution)/shard_map/ppermute | solution.py:383
  16.6 22.9 %collective-permute-start.3 = (f32[256,128]{1,0:T(8,128)S(1)}, f32[256,128]{1,0:T(8,128)S(1)}, u32[]{:S(2)}, u32[]{:S(2)}) collective-permute-start(f32[256,128]{1,0:T(8,128)S(1)} %get-tuple-element.81), channel_id=1, source_target_pairs={{0,31},{1,0},{2,1},{3,2},{4,3},{5,4},{6,5},{7,6},{8,7},{9,8},{10,9... | collective-permute-start | bytes 393224 | tf_op jit(solution)/shard_map/ppermute | solution.py:383
  21.9 19.5 %collective-permute-start.4 = (f32[256,128]{1,0:T(8,128)S(1)}, f32[256,128]{1,0:T(8,128)S(1)}, u32[]{:S(2)}, u32[]{:S(2)}) collective-permute-start(f32[256,128]{1,0:T(8,128)S(1)} %get-tuple-element.82), channel_id=1, source_target_pairs={{0,30},{1,31},{2,0},{3,1},{4,2},{5,3},{6,4},{7,5},{8,6},{9,7},{10,... | collective-permute-start | bytes 393224 | tf_op jit(solution)/shard_map/ppermute | solution.py:383
  22.7 22.6 %collective-permute-start = (f32[256,128]{1,0:T(8,128)S(1)}, f32[256,128]{1,0:T(8,128)S(1)}, u32[]{:S(2)}, u32[]{:S(2)}) collective-permute-start(f32[256,128]{1,0:T(8,128)S(1)} %get-tuple-element.78), channel_id=1, source_target_pairs={{0,1},{1,2},{2,3},{3,4},{4,5},{5,6},{6,7},{7,8},{8,9},{9,10},{10,1... | collective-permute-start | bytes 393224 | tf_op jit(solution)/shard_map/ppermute | solution.py:383
  23.6 21.7 %collective-permute-start.1 = (f32[256,128]{1,0:T(8,128)S(1)}, f32[256,128]{1,0:T(8,128)S(1)}, u32[]{:S(2)}, u32[]{:S(2)}) collective-permute-start(f32[256,128]{1,0:T(8,128)S(1)} %get-tuple-element.79), channel_id=1, source_target_pairs={{0,2},{1,3},{2,4},{3,5},{4,6},{5,7},{6,8},{7,9},{8,10},{9,11},{10,... | collective-permute-start | bytes 393224 | tf_op jit(solution)/shard_map/ppermute | solution.py:383
  34.7 10.5 %copy-start.11 = (f32[9,640]{1,0:T(8,128)S(1)}, f32[9,640]{1,0:T(8,128)}, u32[]{:S(2)}) copy-start(f32[9,640]{1,0:T(8,128)} %param.22) | copy-start | bytes 69124
  34.7 12.8 %copy-start.9 = (f32[4,9,9,640]{3,0,2,1:T(4,128)S(1)}, f32[4,9,9,640]{3,0,2,1:T(4,128)}, u32[]{:S(2)}) copy-start(f32[4,9,9,640]{3,0,2,1:T(4,128)} %param.21) | copy-start | bytes 2488324
  35.9 9.4 %collective-permute-start.5 = (f32[256,128]{1,0:T(8,128)S(1)}, f32[256,128]{1,0:T(8,128)S(1)}, u32[]{:S(2)}, u32[]{:S(2)}) collective-permute-start(f32[256,128]{1,0:T(8,128)S(1)} %get-tuple-element.83), channel_id=1, source_target_pairs={{0,29},{1,30},{2,31},{3,0},{4,1},{5,2},{6,3},{7,4},{8,5},{9,6},{10... | collective-permute-start | bytes 393224 | tf_op jit(solution)/shard_map/ppermute | solution.py:383
  39.5 6.3 %collective-permute-start.6 = (f32[256,128]{1,0:T(8,128)S(1)}, f32[256,128]{1,0:T(8,128)S(1)}, u32[]{:S(2)}, u32[]{:S(2)}) collective-permute-start(f32[256,128]{1,0:T(8,128)S(1)} %get-tuple-element.84), channel_id=1, source_target_pairs={{0,32},{32,64},{64,96},{96,128},{128,160},{160,192},{192,224},{1,3... | collective-permute-start | bytes 393224 | tf_op jit(solution)/shard_map/ppermute | solution.py:387
  41.4 6.1 %collective-permute-start.7 = (f32[256,128]{1,0:T(8,128)S(1)}, f32[256,128]{1,0:T(8,128)S(1)}, u32[]{:S(2)}, u32[]{:S(2)}) collective-permute-start(f32[256,128]{1,0:T(8,128)S(1)} %get-tuple-element.85), channel_id=1, source_target_pairs={{32,0},{64,32},{96,64},{128,96},{160,128},{192,160},{224,192},{33,... | collective-permute-start | bytes 393224 | tf_op jit(solution)/shard_map/ppermute | solution.py:387
  64.6 9.2 %collective-permute-start.10 = (f32[256,128]{1,0:T(8,128)S(1)}, f32[256,128]{1,0:T(8,128)S(1)}, u32[]{:S(2)}, u32[]{:S(2)}) collective-permute-start(f32[256,128]{1,0:T(8,128)S(1)} %get-tuple-element.99), channel_id=1, source_target_pairs={{0,3},{1,4},{2,5},{3,6},{4,7},{5,8},{6,9},{7,10},{8,11},{9,12},{10... | collective-permute-start | bytes 393224 | tf_op jit(solution)/shard_map/ppermute | solution.py:383
  64.7 11.8 %collective-permute-start.11 = (f32[256,128]{1,0:T(8,128)S(1)}, f32[256,128]{1,0:T(8,128)S(1)}, u32[]{:S(2)}, u32[]{:S(2)}) collective-permute-start(f32[256,128]{1,0:T(8,128)S(1)} %get-tuple-element.100), channel_id=1, source_target_pairs={{0,31},{1,0},{2,1},{3,2},{4,3},{5,4},{6,5},{7,6},{8,7},{9,8},{10,9... | collective-permute-start | bytes 393224 | tf_op jit(solution)/shard_map/ppermute | solution.py:383
  70.1 9.0 %collective-permute-start.12 = (f32[256,128]{1,0:T(8,128)S(1)}, f32[256,128]{1,0:T(8,128)S(1)}, u32[]{:S(2)}, u32[]{:S(2)}) collective-permute-start(f32[256,128]{1,0:T(8,128)S(1)} %get-tuple-element.101), channel_id=1, source_target_pairs={{0,30},{1,31},{2,0},{3,1},{4,2},{5,3},{6,4},{7,5},{8,6},{9,7},{10,... | collective-permute-start | bytes 393224 | tf_op jit(solution)/shard_map/ppermute | solution.py:383
  70.9 18.9 %collective-permute-start.13 = (f32[256,128]{1,0:T(8,128)S(1)}, f32[256,128]{1,0:T(8,128)S(1)}, u32[]{:S(2)}, u32[]{:S(2)}) collective-permute-start(f32[256,128]{1,0:T(8,128)S(1)} %get-tuple-element.102), channel_id=1, source_target_pairs={{0,29},{1,30},{2,31},{3,0},{4,1},{5,2},{6,3},{7,4},{8,5},{9,6},{10... | collective-permute-start | bytes 393224 | tf_op jit(solution)/shard_map/ppermute | solution.py:383
  70.9 18.9 %collective-permute-start.14 = (f32[256,128]{1,0:T(8,128)S(1)}, f32[256,128]{1,0:T(8,128)S(1)}, u32[]{:S(2)}, u32[]{:S(2)}) collective-permute-start(f32[256,128]{1,0:T(8,128)S(1)} %get-tuple-element.103), channel_id=1, source_target_pairs={{0,32},{32,64},{64,96},{96,128},{128,160},{160,192},{192,224},{1,3... | collective-permute-start | bytes 393224 | tf_op jit(solution)/shard_map/ppermute | solution.py:387
  73.8 16.0 %collective-permute-start.15 = (f32[256,128]{1,0:T(8,128)S(1)}, f32[256,128]{1,0:T(8,128)S(1)}, u32[]{:S(2)}, u32[]{:S(2)}) collective-permute-start(f32[256,128]{1,0:T(8,128)S(1)} %get-tuple-element.104), channel_id=1, source_target_pairs={{32,0},{64,32},{96,64},{128,96},{160,128},{192,160},{224,192},{33,... | collective-permute-start | bytes 393224 | tf_op jit(solution)/shard_map/ppermute | solution.py:387
  76.5 13.3 %collective-permute-start.8 = (f32[256,128]{1,0:T(8,128)S(1)}, f32[256,128]{1,0:T(8,128)S(1)}, u32[]{:S(2)}, u32[]{:S(2)}) collective-permute-start(f32[256,128]{1,0:T(8,128)S(1)} %get-tuple-element.97), channel_id=1, source_target_pairs={{0,1},{1,2},{2,3},{3,4},{4,5},{5,6},{6,7},{7,8},{8,9},{9,10},{10,1... | collective-permute-start | bytes 393224 | tf_op jit(solution)/shard_map/ppermute | solution.py:383
  79.1 10.8 %collective-permute-start.9 = (f32[256,128]{1,0:T(8,128)S(1)}, f32[256,128]{1,0:T(8,128)S(1)}, u32[]{:S(2)}, u32[]{:S(2)}) collective-permute-start(f32[256,128]{1,0:T(8,128)S(1)} %get-tuple-element.98), channel_id=1, source_target_pairs={{0,2},{1,3},{2,4},{3,5},{4,6},{5,7},{6,8},{7,9},{8,10},{9,11},{10,... | collective-permute-start | bytes 393224 | tf_op jit(solution)/shard_map/ppermute | solution.py:383
  106.9 9.9 %collective-permute-start.18 = (f32[256,128]{1,0:T(8,128)S(1)}, f32[256,128]{1,0:T(8,128)S(1)}, u32[]{:S(2)}, u32[]{:S(2)}) collective-permute-start(f32[256,128]{1,0:T(8,128)S(1)} %get-tuple-element.118), channel_id=1, source_target_pairs={{0,3},{1,4},{2,5},{3,6},{4,7},{5,8},{6,9},{7,10},{8,11},{9,12},{10... | collective-permute-start | bytes 393224 | tf_op jit(solution)/shard_map/ppermute | solution.py:383
  108.8 10.6 %collective-permute-start.19 = (f32[256,128]{1,0:T(8,128)S(1)}, f32[256,128]{1,0:T(8,128)S(1)}, u32[]{:S(2)}, u32[]{:S(2)}) collective-permute-start(f32[256,128]{1,0:T(8,128)S(1)} %get-tuple-element.119), channel_id=1, source_target_pairs={{0,31},{1,0},{2,1},{3,2},{4,3},{5,4},{6,5},{7,6},{8,7},{9,8},{10,9... | collective-permute-start | bytes 393224 | tf_op jit(solution)/shard_map/ppermute | solution.py:383
  112.0 14.2 %collective-permute-start.20 = (f32[256,128]{1,0:T(8,128)S(1)}, f32[256,128]{1,0:T(8,128)S(1)}, u32[]{:S(2)}, u32[]{:S(2)}) collective-permute-start(f32[256,128]{1,0:T(8,128)S(1)} %get-tuple-element.120), channel_id=1, source_target_pairs={{0,30},{1,31},{2,0},{3,1},{4,2},{5,3},{6,4},{7,5},{8,6},{9,7},{10,... | collective-permute-start | bytes 393224 | tf_op jit(solution)/shard_map/ppermute | solution.py:383
  113.2 23.7 %collective-permute-start.16 = (f32[256,128]{1,0:T(8,128)S(1)}, f32[256,128]{1,0:T(8,128)S(1)}, u32[]{:S(2)}, u32[]{:S(2)}) collective-permute-start(f32[256,128]{1,0:T(8,128)S(1)} %get-tuple-element.116), channel_id=1, source_target_pairs={{0,1},{1,2},{2,3},{3,4},{4,5},{5,6},{6,7},{7,8},{8,9},{9,10},{10,1... | collective-permute-start | bytes 393224 | tf_op jit(solution)/shard_map/ppermute | solution.py:383
  113.3 23.7 %collective-permute-start.17 = (f32[256,128]{1,0:T(8,128)S(1)}, f32[256,128]{1,0:T(8,128)S(1)}, u32[]{:S(2)}, u32[]{:S(2)}) collective-permute-start(f32[256,128]{1,0:T(8,128)S(1)} %get-tuple-element.117), channel_id=1, source_target_pairs={{0,2},{1,3},{2,4},{3,5},{4,6},{5,7},{6,8},{7,9},{8,10},{9,11},{10,... | collective-permute-start | bytes 393224 | tf_op jit(solution)/shard_map/ppermute | solution.py:383
  116.7 20.2 %collective-permute-start.21 = (f32[256,128]{1,0:T(8,128)S(1)}, f32[256,128]{1,0:T(8,128)S(1)}, u32[]{:S(2)}, u32[]{:S(2)}) collective-permute-start(f32[256,128]{1,0:T(8,128)S(1)} %get-tuple-element.121), channel_id=1, source_target_pairs={{0,29},{1,30},{2,31},{3,0},{4,1},{5,2},{6,3},{7,4},{8,5},{9,6},{10... | collective-permute-start | bytes 393224 | tf_op jit(solution)/shard_map/ppermute | solution.py:383
  119.4 17.5 %collective-permute-start.22 = (f32[256,128]{1,0:T(8,128)S(1)}, f32[256,128]{1,0:T(8,128)S(1)}, u32[]{:S(2)}, u32[]{:S(2)}) collective-permute-start(f32[256,128]{1,0:T(8,128)S(1)} %get-tuple-element.122), channel_id=1, source_target_pairs={{0,32},{32,64},{64,96},{96,128},{128,160},{160,192},{192,224},{1,3... | collective-permute-start | bytes 393224 | tf_op jit(solution)/shard_map/ppermute | solution.py:387
  126.2 10.8 %collective-permute-start.23 = (f32[256,128]{1,0:T(8,128)S(1)}, f32[256,128]{1,0:T(8,128)S(1)}, u32[]{:S(2)}, u32[]{:S(2)}) collective-permute-start(f32[256,128]{1,0:T(8,128)S(1)} %get-tuple-element.123), channel_id=1, source_target_pairs={{32,0},{64,32},{96,64},{128,96},{160,128},{192,160},{224,192},{33,... | collective-permute-start | bytes 393224 | tf_op jit(solution)/shard_map/ppermute | solution.py:387
  137.0 12.5 %copy-start.12 = (s32[16]{0:T(128)S(1)}, s32[16]{0:T(128)}, u32[]{:S(2)}) copy-start(s32[16]{0:T(128)} %param.28) | copy-start | bytes 196

commit v2 on v1

--- a/solution.py
+++ b/solution.py
@@ -121,8 +121,9 @@
     lane = lax.broadcasted_iota(jnp.int32, (SEND_ROWS, LANES), 1) < HALF
     tail = SEND_ROWS - (rows - SEND_ROWS)
     pairs = len(message_refs) // 2
-    receivers = weight_ref.shape[1]
-    if not pairs:
+    if values_ref is None:
+        picked = pick(field, select_ref[:, : pairs * LANES])
+    elif not pairs:
         picked = pick(field, select_ref[:, select_ref.shape[1] - LANES :])
     else:
         picked = pick(field, select_ref[...])
@@ -132,6 +133,9 @@
         bottom = jnp.concatenate([block[SEND_ROWS:], jnp.zeros((tail, LANES), F32)], 0)
         message_refs[2 * pair][...] = jnp.where(lane, top, pltpu.roll(bottom, HALF, 1))
         message_refs[2 * pair + 1][...] = jnp.where(lane, pltpu.roll(top, HALF, 1), bottom)
+    if values_ref is None:
+        return
+    receivers = weight_ref.shape[1]
     block = picked[:, pairs * LANES : pairs * LANES + receivers]
     for q in range(quantities):
         values_ref[q : q + 1, :] = jnp.sum(
@@ -139,10 +143,9 @@
         )
 
 
-def first_kernel(count_ref, field_ref, send_ref, receiver_ref, weight_ref, select_ref, *messages):
+def first_kernel(quantities, count_ref, field_ref, send_ref, receiver_ref, select_ref, *messages):
     rows = field_ref.shape[0]
     width = select_ref.shape[0]
-    basis = weight_ref.shape[0]
     slots, capacity = send_ref.shape
     receivers = receiver_ref.shape[1]
     select_ref[:, slots * capacity :] = jnp.zeros((width, LANES), BF16)
@@ -159,8 +162,7 @@
     select_ref[:, slots * capacity : slots * capacity + receivers] = jnp.where(
         element == receiver_ref[...], 1.0, 0.0
     ).astype(BF16)
-    values_ref = messages[-1]
-    pack(field_ref[...], select_ref, weight_ref, messages[:-1], values_ref, rows // basis, basis)
+    pack(field_ref[...], select_ref, None, messages, None, quantities, rows // quantities)
 
 
 def own_maps(star_ref, local_ref, terms_ref):
@@ -356,14 +358,14 @@
     gathered_shape = jax.ShapeDtypeStruct((faces, rows, width), F32)
     select_shape = jax.ShapeDtypeStruct((width + LANES, halo_width + LANES), BF16)
     outs = pl.pallas_call(
-        first_kernel,
-        out_shape=(select_shape,) + (message,) * slots + (values_shape,),
-        in_specs=smem(1) + vmem(4),
-        out_specs=tuple(vmem(slots + 2)),
+        lambda *refs: first_kernel(quantities, *refs),
+        out_shape=(select_shape,) + (message,) * slots,
+        in_specs=smem(1) + vmem(3),
+        out_specs=tuple(vmem(slots + 1)),
         name="first_messages",
         **granted(16),
-    )(send_count, fields, send_element[0], receiver_element[None, :], receiver_weight)
-    select, messages = outs[0], outs[1:-1]
+    )(send_count, fields, send_element[0], receiver_element[None, :])
+    select, messages = outs[0], outs[1:]
 
     element_row = jnp.arange(width + LANES, dtype=jnp.int32)[:, None]
     element_row = jnp.where(element_row < width, element_row, element_row - LANES)

time: 170 us -> 189 us (1.11)
  local copies, waits for them, and re-layouts: 5.79 us -> 22.5 us
    unnamed x28 -> x68, local copies, waits for them, and re-layouts: 5.05 us -> 21.7 us
  transfers between devices with their start and end apart: 24 -> 24, of which waited for: 6 -> 5; matrix products, arithmetic and copies ran while one was open for 1% -> 2% of each run, Pallas kernels for 15% -> 14%
where the time goes in v2:
time: 189 us
  Pallas kernels  80.5 us (43%)
  starting transfers between devices  52 us (28%)
  local copies, waits for them, and re-layouts  22.5 us (12%)
  blocking collectives  17.6 us (9%)
  waiting for transfers between devices  9.31 us (5%)
  other arithmetic  4.84 us (3%)
    pallas_call x3, Pallas kernels, per_device(): pl.pallas_call(lambda *refs, sends=sends: halo_kernel(slots, sends, *refs...  37.9 us
    ppermute x18, starting transfers between devices, send(): return lax.ppermute(value, 'dom', pairs)  37.1 us
    pallas_call x3, Pallas kernels, per_device(): pl.pallas_call(own_kernel_b, out_shape=(jax.ShapeDtypeStruct((rows, width...  25.5 us
    unnamed x68, local copies, waits for them, and re-layouts  21.7 us
    all_to_all x1, blocking collectives, per_device(): lax.all_to_all(pieces, 'dom', split_axis=0, concat_axis=0, tiled=True)  17.6 us
    ppermute x6, starting transfers between devices, send(): return lax.ppermute(value, 'grp', pairs)  14.9 us
    pallas_call x3, Pallas kernels, per_device(): pl.pallas_call(own_kernel_a, out_shape=(terms_shape, parts_shape, parts_s...  14.4 us
    ppermute x18, waiting for transfers between devices, send(): return lax.ppermute(value, 'dom', pairs)  6.85 us
  transfers between devices with their start and end apart: 24, of which 5 were waited for; matrix products, arithmetic and copies ran while one was open for 2% of the time, Pallas kernels for 14%

profile of v2, /device:TPU:16, one launch (start us, length us, event | category | flops | bytes accessed | tf_op | source)
XLA Modules:
  0.0 188.7 jit_solution(10246872235571359496)
XLA Ops:
  0.6 1.0 pad_maximum_fusion
  2.0 1.1 copy-done.2
  3.1 1.1 copy-done.4
  4.3 1.3 copy-done.6
  5.6 4.8 %own_terms_a.3 = (f32[7,504,640]{2,1,0:T(8,128)S(1)}, bf16[4,504,640]{2,1,0:T(8,128)(2,1)S(1)}, bf16[4,504,640]{2,1,0:T(8,128)(2,1)S(1)}, f32[504,128]{1,0:T(8,128)S(1)}) custom-call(f32[504,640]{1,0:T(8,128)S(1)} %bitcast.39, bf16[616,192]{1,0:T(8,128)(2,1)S(1)} %add_convert_fusion.matrix_ref, f32[9,9,3,640]{3,2,1,0:T(4,128)S(1)} %bitcast.27, ...), custom_call_target="tpu_custom_call" | custom-call | flops 5000000000 | bytes 8000000 | tf_op jit(solution)/shard_map/own_terms_a/pallas_call | solution.py:398
  11.1 2.7 %first_messages.1 = (bf16[768,640]{1,0:T(8,128)(2,1)S(1)}, f32[256,128]{1,0:T(8,128)}, f32[256,128]{1,0:T(8,128)}, f32[256,128]{1,0:T(8,128)S(1)}, f32[256,128]{...) custom-call(s32[1,8]{1,0:T(1,128)S(1)} %copy-done.11, ...), custom_call_target="tpu_custom_call" | custom-call | tf_op jit(solution)/shard_map/first_messages/pallas_call | solution.py:360
  13.8 1.0 copy-done.17
  14.8 2.8 %collective-permute-start.2 = (f32[256,128]{1,0:T(8,128)S(1)}, f32[256,128]{1,0:T(8,128)S(1)}, u32[]{:S(2)}, u32[]{:S(2)}) collective-permute-start(f32[256,128]{1,0:T(8,128)S(1)} %get-tuple-element.80), channel_id=1, source_target_pairs={{0,3},{1,4},{2,5},{3,6},{4,7},{5,8},{6,9},{7,10},{8,11},{9,12},{10... | collective-permute-start | bytes 393224 | tf_op jit(solution)/shard_map/ppermute | solution.py:385
  17.6 5.3 %collective-permute-start.3 = (f32[256,128]{1,0:T(8,128)S(1)}, f32[256,128]{1,0:T(8,128)S(1)}, u32[]{:S(2)}, u32[]{:S(2)}) collective-permute-start(f32[256,128]{1,0:T(8,128)S(1)} %get-tuple-element.81), channel_id=1, source_target_pairs={{0,31},{1,0},{2,1},{3,2},{4,3},{5,4},{6,5},{7,6},{8,7},{9,8},{10,9... | collective-permute-start | bytes 393224 | tf_op jit(solution)/shard_map/ppermute | solution.py:385
  24.6 1.9 collective-permute-start.1
  27.2 8.5 %own_terms_b.3 = (f32[504,512]{1,0:T(8,128)S(1)}, f32[4,504,640]{2,1,0:T(8,128)S(1)}) custom-call(f32[504,640]{1,0:T(8,128)S(1)} %bitcast.41, f32[7,504,640]{2,1,0:T(8,128)S(1)} %get-tuple-element.67.terms_ref, f32[9,9,3,640]{3,2,1,0:T(4,128)S(1)} %bitcast.28, f32[9,9,4,640]{3,2,1,0:T(4,128)S(1)} %bitcast.34, ...), custom_call_target="tpu_custom_call" | custom-call | flops 5000000000 | bytes 8000000 | tf_op jit(solution)/shard_map/own_terms_b/pallas_call | solution.py:412
  35.7 2.3 %copy-done.13 = f32[4,504,640]{2,1,0:T(8,128)} copy-done((f32[4,504,640]{2,1,0:T(8,128)}, f32[4,504,640]{2,1,0:T(8,128)S(1)}, u32[]{:S(2)}) %copy-start.13) | copy-done | bytes 5160984
  38.0 2.0 %compare_convert_fusion.1.refs_7_ = bf16[4,512,640]{2,1,0:T(8,128)(2,1)} fusion(s32[4,640]{1,0:T(4,128)S(1)} %copy-done.29, s32[512]{0:T(512)S(1)} %iota_add_fusion), kind=kLoop, calls=%fused_computation.1 | loop fusion | flops 2621440 | bytes 2633728 | tf_op jit(solution)/shard_map/convert_element_type | solution.py:374
  41.3 3.5 %collective-permute-start.5 = (f32[256,128]{1,0:T(8,128)}, f32[256,128]{1,0:T(8,128)}, u32[]{:S(2)}, u32[]{:S(2)}) collective-permute-start(f32[256,128]{1,0:T(8,128)} %get-tuple-element.83), channel_id=1, source_target_pairs={{0,29},{1,30},{2,31},{3,0},{4,1},{5,2},{6,3},{7,4},{8,5},{9,6},{10... | collective-permute-start | bytes 393224 | tf_op jit(solution)/shard_map/ppermute | solution.py:385
  45.5 1.9 %collective-permute-start.6 = (f32[256,128]{1,0:T(8,128)}, f32[256,128]{1,0:T(8,128)}, u32[]{:S(2)}, u32[]{:S(2)}) collective-permute-start(f32[256,128]{1,0:T(8,128)} %get-tuple-element.84), channel_id=1, source_target_pairs={{0,32},{32,64},{64,96},{96,128},{128,160},{160,192},{192,224},{1,3... | collective-permute-start | bytes 393224 | tf_op jit(solution)/shard_map/ppermute | solution.py:389
  48.0 3.8 %collective-permute-start.7 = (f32[256,128]{1,0:T(8,128)}, f32[256,128]{1,0:T(8,128)}, u32[]{:S(2)}, u32[]{:S(2)}) collective-permute-start(f32[256,128]{1,0:T(8,128)} %get-tuple-element.85), channel_id=1, source_target_pairs={{32,0},{64,32},{96,64},{128,96},{160,128},{192,160},{224,192},{33,... | collective-permute-start | bytes 393224 | tf_op jit(solution)/shard_map/ppermute | solution.py:389
  52.1 2.4 %collective-permute-done.7.refs_18_ = f32[256,128]{1,0:T(8,128)} collective-permute-done((f32[256,128]{1,0:T(8,128)}, f32[256,128]{1,0:T(8,128)}, u32[]{:S(2)}, u32[]{:S(2)}) %collective-permute-start.7) | collective-permute-done | bytes 131104 | tf_op jit(solution)/shard_map/ppermute | solution.py:389
  54.5 1.7 copy-done.8
  56.2 2.5 %copy-done.14 = f32[4,504,640]{2,1,0:T(8,128)S(1)} copy-done((f32[4,504,640]{2,1,0:T(8,128)S(1)}, f32[4,504,640]{2,1,0:T(8,128)}, u32[]{:S(2)}) %copy-start.14) | copy-done | bytes 5160984
  58.7 1.2 copy-done.16
  59.9 1.2 copy-done.18
  61.1 1.1 copy-done.19
  62.3 0.9 copy-done.22
  63.2 0.9 copy-done.24
  64.1 0.9 copy-done.26
  65.0 0.9 copy-done.28
  65.9 13.3 %halo_terms.2 = (f32[504,640]{1,0:T(8,128)S(1)}, f32[8,128]{1,0:T(8,128)S(1)}, f32[9,16]{1,0:T(8,128)S(1)}, f32[256,128]{1,0:T(8,128)S(1)}, f32[256,128]{1,0:T(8...) custom-call(f32[1,640]{1,0:T(1,128)S(1)} %compare_convert_fusion.2.r, ...), custom_call_target="tpu_custom_call" | custom-call | flops 6000000000 | bytes 8000000 | tf_op jit(solution)/shard_map/halo_terms/pallas_call | solution.py:421
  79.3 4.8 %own_terms_a.4 = (f32[7,504,640]{2,1,0:T(8,128)S(1)}, bf16[4,504,640]{2,1,0:T(8,128)(2,1)S(1)}, bf16[4,504,640]{2,1,0:T(8,128)(2,1)S(1)}, f32[504,128]{1,0:T(8,128)S(1)}) custom-call(f32[504,640]{1,0:T(8,128)S(1)} %get-tuple-element.86.field_ref.refs_1_, bf16[616,192]{1,0:T(8,128)(2,1)S(1)} %add_convert_fusion.matrix_ref, f32[9,9,3,640]{3,2,1,0:T(4,128)S(1)} %bitcast.29, ...), custom_call_target="tpu_custom_call" | custom-call | flops 5000000000 | bytes 8000000 | tf_op jit(solution)/shard_map/own_terms_a/pallas_call | solution.py:398
  84.2 5.4 %collective-permute-start.11 = (f32[256,128]{1,0:T(8,128)S(1)}, f32[256,128]{1,0:T(8,128)S(1)}, u32[]{:S(2)}, u32[]{:S(2)}) collective-permute-start(f32[256,128]{1,0:T(8,128)S(1)} %get-tuple-element.100), channel_id=1, source_target_pairs={{0,31},{1,0},{2,1},{3,2},{4,3},{5,4},{6,5},{7,6},{8,7},{9,8},{10,9... | collective-permute-start | bytes 393224 | tf_op jit(solution)/shard_map/ppermute | solution.py:385
  90.4 2.5 %collective-permute-start.14 = (f32[256,128]{1,0:T(8,128)S(1)}, f32[256,128]{1,0:T(8,128)S(1)}, u32[]{:S(2)}, u32[]{:S(2)}) collective-permute-start(f32[256,128]{1,0:T(8,128)S(1)} %get-tuple-element.103), channel_id=1, source_target_pairs={{0,32},{32,64},{64,96},{96,128},{128,160},{160,192},{192,224},{1,3... | collective-permute-start | bytes 393224 | tf_op jit(solution)/shard_map/ppermute | solution.py:389
  93.4 2.6 %collective-permute-start.15 = (f32[256,128]{1,0:T(8,128)S(1)}, f32[256,128]{1,0:T(8,128)S(1)}, u32[]{:S(2)}, u32[]{:S(2)}) collective-permute-start(f32[256,128]{1,0:T(8,128)S(1)} %get-tuple-element.104), channel_id=1, source_target_pairs={{32,0},{64,32},{96,64},{128,96},{160,128},{192,160},{224,192},{33,... | collective-permute-start | bytes 393224 | tf_op jit(solution)/shard_map/ppermute | solution.py:389
  96.0 2.1 %collective-permute-start.8 = (f32[256,128]{1,0:T(8,128)S(1)}, f32[256,128]{1,0:T(8,128)S(1)}, u32[]{:S(2)}, u32[]{:S(2)}) collective-permute-start(f32[256,128]{1,0:T(8,128)S(1)} %get-tuple-element.97), channel_id=1, source_target_pairs={{0,1},{1,2},{2,3},{3,4},{4,5},{5,6},{6,7},{7,8},{8,9},{9,10},{10,1... | collective-permute-start | bytes 393224 | tf_op jit(solution)/shard_map/ppermute | solution.py:385
  98.5 2.2 %collective-permute-start.9 = (f32[256,128]{1,0:T(8,128)S(1)}, f32[256,128]{1,0:T(8,128)S(1)}, u32[]{:S(2)}, u32[]{:S(2)}) collective-permute-start(f32[256,128]{1,0:T(8,128)S(1)} %get-tuple-element.98), channel_id=1, source_target_pairs={{0,2},{1,3},{2,4},{3,5},{4,6},{5,7},{6,8},{7,9},{8,10},{9,11},{10,... | collective-permute-start | bytes 393224 | tf_op jit(solution)/shard_map/ppermute | solution.py:385
  100.8 8.5 %own_terms_b.4 = (f32[504,512]{1,0:T(8,128)S(1)}, f32[4,504,640]{2,1,0:T(8,128)S(1)}) custom-call(f32[504,640]{1,0:T(8,128)S(1)} %get-tuple-element.86.field_ref.refs_1_, f32[7,504,640]{2,1,0:T(8,128)S(1)} %get-tuple-element.87.terms_ref, f32[9,9,3,640]{3,2,1,0:T(4,128)S(1)} %bitcast.30, f32[9,9,4,640]{3,2,1,0:T(4,128)S(1)} %bitcast.36, ...), custom_call_target="tpu_custom_call" | custom-call | flops 5000000000 | bytes 8000000 | tf_op jit(solution)/shard_map/own_terms_b/pallas_call | solution.py:412
  109.4 12.2 %halo_terms.3 = (f32[504,640]{1,0:T(8,128)S(1)}, f32[8,128]{1,0:T(8,128)S(1)}, f32[9,16]{1,0:T(8,128)S(1)}, f32[256,128]{1,0:T(8,128)S(1)}, f32[256,128]{1,0:T(8...) custom-call(f32[1,640]{1,0:T(1,128)S(1)} %compare_convert_fusion.2.r, ...), custom_call_target="tpu_custom_call" | custom-call | flops 6000000000 | bytes 8000000 | tf_op jit(solution)/shard_map/halo_terms/pallas_call | solution.py:421
  121.6 4.8 %own_terms_a.5 = (f32[7,504,640]{2,1,0:T(8,128)S(1)}, bf16[4,504,640]{2,1,0:T(8,128)(2,1)S(1)}, bf16[4,504,640]{2,1,0:T(8,128)(2,1)S(1)}, f32[504,128]{1,0:T(8,128)S(1)}) custom-call(f32[504,640]{1,0:T(8,128)S(1)} %get-tuple-element.105.field_ref.refs_1_, bf16[616,192]{1,0:T(8,128)(2,1)S(1)} %add_convert_fusion.matrix_ref, f32[9,9,3,640]{3,2,1,0:T(4,128)S(1)} %bitcast.31, ...), custom_call_target="tpu_custom_call" | custom-call | flops 5000000000 | bytes 8000000 | tf_op jit(solution)/shard_map/own_terms_a/pallas_call | solution.py:398
  126.4 2.0 %collective-permute-start.18 = (f32[256,128]{1,0:T(8,128)S(1)}, f32[256,128]{1,0:T(8,128)S(1)}, u32[]{:S(2)}, u32[]{:S(2)}) collective-permute-start(f32[256,128]{1,0:T(8,128)S(1)} %get-tuple-element.118), channel_id=1, source_target_pairs={{0,3},{1,4},{2,5},{3,6},{4,7},{5,8},{6,9},{7,10},{8,11},{9,12},{10... | collective-permute-start | bytes 393224 | tf_op jit(solution)/shard_map/ppermute | solution.py:385
  128.4 3.2 %collective-permute-start.19 = (f32[256,128]{1,0:T(8,128)S(1)}, f32[256,128]{1,0:T(8,128)S(1)}, u32[]{:S(2)}, u32[]{:S(2)}) collective-permute-start(f32[256,128]{1,0:T(8,128)S(1)} %get-tuple-element.119), channel_id=1, source_target_pairs={{0,31},{1,0},{2,1},{3,2},{4,3},{5,4},{6,5},{7,6},{8,7},{9,8},{10,9... | collective-permute-start | bytes 393224 | tf_op jit(solution)/shard_map/ppermute | solution.py:385
  131.6 1.1 collective-permute-start.20
  132.8 2.5 %collective-permute-start.17 = (f32[256,128]{1,0:T(8,128)S(1)}, f32[256,128]{1,0:T(8,128)S(1)}, u32[]{:S(2)}, u32[]{:S(2)}) collective-permute-start(f32[256,128]{1,0:T(8,128)S(1)} %get-tuple-element.117), channel_id=1, source_target_pairs={{0,2},{1,3},{2,4},{3,5},{4,6},{5,7},{6,8},{7,9},{8,10},{9,11},{10,... | collective-permute-start | bytes 393224 | tf_op jit(solution)/shard_map/ppermute | solution.py:385
  135.3 1.0 collective-permute-done.18.refs_13_
  136.3 2.7 %collective-permute-start.21 = (f32[256,128]{1,0:T(8,128)S(1)}, f32[256,128]{1,0:T(8,128)S(1)}, u32[]{:S(2)}, u32[]{:S(2)}) collective-permute-start(f32[256,128]{1,0:T(8,128)S(1)} %get-tuple-element.121), channel_id=1, source_target_pairs={{0,29},{1,30},{2,31},{3,0},{4,1},{5,2},{6,3},{7,4},{8,5},{9,6},{10... | collective-permute-start | bytes 393224 | tf_op jit(solution)/shard_map/ppermute | solution.py:385
  139.0 1.9 %collective-permute-start.22 = (f32[256,128]{1,0:T(8,128)S(1)}, f32[256,128]{1,0:T(8,128)S(1)}, u32[]{:S(2)}, u32[]{:S(2)}) collective-permute-start(f32[256,128]{1,0:T(8,128)S(1)} %get-tuple-element.122), channel_id=1, source_target_pairs={{0,32},{32,64},{64,96},{96,128},{128,160},{160,192},{192,224},{1,3... | collective-permute-start | bytes 393224 | tf_op jit(solution)/shard_map/ppermute | solution.py:389
  140.9 4.9 %collective-permute-done.20.refs_15_ = f32[256,128]{1,0:T(8,128)S(1)} collective-permute-done((f32[256,128]{1,0:T(8,128)S(1)}, f32[256,128]{1,0:T(8,128)S(1)}, u32[]{:S(2)}, u32[]{:S(2)}) %collective-permute-start.20) | collective-permute-done | bytes 131104 | tf_op jit(solution)/shard_map/ppermute | solution.py:385
  145.8 2.2 %collective-permute-start.23 = (f32[256,128]{1,0:T(8,128)S(1)}, f32[256,128]{1,0:T(8,128)S(1)}, u32[]{:S(2)}, u32[]{:S(2)}) collective-permute-start(f32[256,128]{1,0:T(8,128)S(1)} %get-tuple-element.123), channel_id=1, source_target_pairs={{32,0},{64,32},{96,64},{128,96},{160,128},{192,160},{224,192},{33,... | collective-permute-start | bytes 393224 | tf_op jit(solution)/shard_map/ppermute | solution.py:389
  148.0 8.5 %own_terms_b.5 = (f32[504,512]{1,0:T(8,128)S(1)}, f32[4,504,640]{2,1,0:T(8,128)S(1)}) custom-call(f32[504,640]{1,0:T(8,128)S(1)} %get-tuple-element.105.field_ref.refs_1_, f32[7,504,640]{2,1,0:T(8,128)S(1)} %get-tuple-element.106.terms_ref, f32[9,9,3,640]{3,2,1,0:T(4,128)S(1)} %bitcast.32, f32[9,9,4,640]{3,2,1,0:T(4,128)S(1)} %bitcast.38, ...), custom_call_target="tpu_custom_call" | custom-call | flops 5000000000 | bytes 8000000 | tf_op jit(solution)/shard_map/own_terms_b/pallas_call | solution.py:412
  156.5 12.3 %halo_terms_last.1 = (f32[504,640]{1,0:T(8,128)}, f32[8,128]{1,0:T(8,128)S(1)}, f32[9,16]{1,0:T(8,128)S(1)}) custom-call(f32[1,640]{1,0:T(1,128)S(1)} %compare_convert_fusion.2.refs_0_, f32[504,640]{1,0:T(8,128)S(1)} %get-tuple-element.105.field_ref.refs_1_, f32[504,512]{1,0:T(8,128)S(1)} %get-tuple-element.109.refs_2_, ...), custom_call_target="tpu_custom_call" | custom-call | flops 6000000000 | bytes 8000000 | tf_op jit(solution)/shard_map/halo_terms_last/pallas_call | solution.py:421
  169.8 17.6 %all_to_all.9 = f32[32,1,448]{2,1,0:T(1,128)S(1)} all-to-all(f32[32,1,448]{2,1,0:T(1,128)S(1)} %all_to_all.6), channel_id=1, replica_groups=mesh['grp'=8,'dom'=32] {'dom'}, dimensions={0} | all-to-all | bytes 114688 | tf_op jit(solution)/shard_map/all_to_all | solution.py:449
  (104 shorter events, 9.8 us)
Async XLA Ops:
  2.0 1.2 copy-start.2
  3.1 1.1 copy-start.4
  4.3 1.3 copy-start.6
  5.6 5.5 %copy-start.7 = (f32[56,9,640]{2,0,1:T(8,128)S(1)}, f32[56,9,640]{2,0,1:T(8,128)}, u32[]{:S(2)}) copy-start(f32[56,9,640]{2,0,1:T(8,128)} %param.15) | copy-start | bytes 3870724
  5.6 5.5 %copy-start.10 = (s32[1,8,64]{2,1,0:T(8,128)S(1)}, s32[1,8,64]{2,1,0:T(8,128)}, u32[]{:S(2)}) copy-start(s32[1,8,64]{2,1,0:T(8,128)} %param.26) | copy-start | bytes 6148
  5.6 5.5 %copy-start.11 = (s32[1,8]{1,0:T(1,128)S(1)}, s32[1,8]{1,0:T(1,128)}, u32[]{:S(2)}) copy-start(s32[1,8]{1,0:T(1,128)} %refs_0_.1) | copy-start | bytes 100
  5.6 5.5 %copy-start.12 = (s32[16]{0:T(128)S(1)}, s32[16]{0:T(128)}, u32[]{:S(2)}) copy-start(s32[16]{0:T(128)} %param.27) | copy-start | bytes 196
  5.6 20.8 %copy-start.29 = (s32[4,640]{1,0:T(4,128)S(1)}, s32[4,640]{1,0:T(4,128)}, u32[]{:S(2)}) copy-start(s32[4,640]{1,0:T(4,128)} %param.23) | copy-start | bytes 30724
  11.1 16.0 %copy-start.3 = (f32[3,9,9,640]{3,0,2,1:T(4,128)S(1)}, f32[3,9,9,640]{3,0,2,1:T(4,128)}, u32[]{:S(2)}) copy-start(f32[3,9,9,640]{3,0,2,1:T(4,128)} %param.19) | copy-start | bytes 1866244
  11.1 16.0 %copy-start.5 = (f32[4,9,9,640]{3,0,2,1:T(4,128)S(1)}, f32[4,9,9,640]{3,0,2,1:T(4,128)}, u32[]{:S(2)}) copy-start(f32[4,9,9,640]{3,0,2,1:T(4,128)} %param.20) | copy-start | bytes 2488324
  14.8 25.8 %collective-permute-start.2 = (f32[256,128]{1,0:T(8,128)S(1)}, f32[256,128]{1,0:T(8,128)S(1)}, u32[]{:S(2)}, u32[]{:S(2)}) collective-permute-start(f32[256,128]{1,0:T(8,128)S(1)} %get-tuple-element.80), channel_id=1, source_target_pairs={{0,3},{1,4},{2,5},{3,6},{4,7},{5,8},{6,9},{7,10},{8,11},{9,12},{10... | collective-permute-start | bytes 393224 | tf_op jit(solution)/shard_map/ppermute | solution.py:385
  17.6 27.2 %collective-permute-start.3 = (f32[256,128]{1,0:T(8,128)S(1)}, f32[256,128]{1,0:T(8,128)S(1)}, u32[]{:S(2)}, u32[]{:S(2)}) collective-permute-start(f32[256,128]{1,0:T(8,128)S(1)} %get-tuple-element.81), channel_id=1, source_target_pairs={{0,31},{1,0},{2,1},{3,2},{4,3},{5,4},{6,5},{7,6},{8,7},{9,8},{10,9... | collective-permute-start | bytes 393224 | tf_op jit(solution)/shard_map/ppermute | solution.py:385
  22.9 24.5 %collective-permute-start.4 = (f32[256,128]{1,0:T(8,128)S(1)}, f32[256,128]{1,0:T(8,128)S(1)}, u32[]{:S(2)}, u32[]{:S(2)}) collective-permute-start(f32[256,128]{1,0:T(8,128)S(1)} %get-tuple-element.82), channel_id=1, source_target_pairs={{0,30},{1,31},{2,0},{3,1},{4,2},{5,3},{6,4},{7,5},{8,6},{9,7},{10,... | collective-permute-start | bytes 393224 | tf_op jit(solution)/shard_map/ppermute | solution.py:385
  23.7 28.3 %collective-permute-start = (f32[256,128]{1,0:T(8,128)}, f32[256,128]{1,0:T(8,128)}, u32[]{:S(2)}, u32[]{:S(2)}) collective-permute-start(f32[256,128]{1,0:T(8,128)} %get-tuple-element.78), channel_id=1, source_target_pairs={{0,1},{1,2},{2,3},{3,4},{4,5},{5,6},{6,7},{7,8},{8,9},{9,10},{10,1... | collective-permute-start | bytes 393224 | tf_op jit(solution)/shard_map/ppermute | solution.py:385
  24.6 27.5 %collective-permute-start.1 = (f32[256,128]{1,0:T(8,128)}, f32[256,128]{1,0:T(8,128)}, u32[]{:S(2)}, u32[]{:S(2)}) collective-permute-start(f32[256,128]{1,0:T(8,128)} %get-tuple-element.79), channel_id=1, source_target_pairs={{0,2},{1,3},{2,4},{3,5},{4,6},{5,7},{6,8},{7,9},{8,10},{9,11},{10,... | collective-permute-start | bytes 393224 | tf_op jit(solution)/shard_map/ppermute | solution.py:385
  27.2 8.5 %copy-start = (bf16[4,768,640]{2,1,0:T(8,128)(2,1)}, bf16[4,768,640]{2,1,0:T(8,128)(2,1)S(1)}, u32[]{:S(2)}) copy-start(bf16[4,768,640]{2,1,0:T(8,128)(2,1)S(1)} %compare_convert_fusion.choose_ref) | copy-start | bytes 11796484
  35.7 2.3 %copy-start.13 = (f32[4,504,640]{2,1,0:T(8,128)}, f32[4,504,640]{2,1,0:T(8,128)S(1)}, u32[]{:S(2)}) copy-start(f32[4,504,640]{2,1,0:T(8,128)S(1)} %get-tuple-element.76.refs_4_) | copy-start | bytes 15482884
  38.0 13.9 %copy-start.15 = (f32[504,512]{1,0:T(8,128)}, f32[504,512]{1,0:T(8,128)S(1)}, u32[]{:S(2)}) copy-start(f32[504,512]{1,0:T(8,128)S(1)} %get-tuple-element.70.refs_2_) | copy-start | bytes 3096580
  38.0 13.9 %copy-start.30 = (f32[9,640]{1,0:T(8,128)S(1)}, f32[9,640]{1,0:T(8,128)}, u32[]{:S(2)}) copy-start(f32[9,640]{1,0:T(8,128)} %param.22) | copy-start | bytes 69124
  38.0 13.9 %copy-start.31 = (f32[56,16]{0,1:T(8,128)S(1)}, f32[56,16]{0,1:T(8,128)}, u32[]{:S(2)}) copy-start(f32[56,16]{0,1:T(8,128)} %param.29) | copy-start | bytes 10756
  41.3 10.7 %collective-permute-start.5 = (f32[256,128]{1,0:T(8,128)}, f32[256,128]{1,0:T(8,128)}, u32[]{:S(2)}, u32[]{:S(2)}) collective-permute-start(f32[256,128]{1,0:T(8,128)} %get-tuple-element.83), channel_id=1, source_target_pairs={{0,29},{1,30},{2,31},{3,0},{4,1},{5,2},{6,3},{7,4},{8,5},{9,6},{10... | collective-permute-start | bytes 393224 | tf_op jit(solution)/shard_map/ppermute | solution.py:385
  45.5 6.6 %collective-permute-start.6 = (f32[256,128]{1,0:T(8,128)}, f32[256,128]{1,0:T(8,128)}, u32[]{:S(2)}, u32[]{:S(2)}) collective-permute-start(f32[256,128]{1,0:T(8,128)} %get-tuple-element.84), channel_id=1, source_target_pairs={{0,32},{32,64},{64,96},{96,128},{128,160},{160,192},{192,224},{1,3... | collective-permute-start | bytes 393224 | tf_op jit(solution)/shard_map/ppermute | solution.py:389
  48.0 6.5 %collective-permute-start.7 = (f32[256,128]{1,0:T(8,128)}, f32[256,128]{1,0:T(8,128)}, u32[]{:S(2)}, u32[]{:S(2)}) collective-permute-start(f32[256,128]{1,0:T(8,128)} %get-tuple-element.85), channel_id=1, source_target_pairs={{32,0},{64,32},{96,64},{128,96},{160,128},{192,160},{224,192},{33,... | collective-permute-start | bytes 393224 | tf_op jit(solution)/shard_map/ppermute | solution.py:389
  54.5 1.7 copy-start.8
  56.2 2.5 %copy-start.14 = (f32[4,504,640]{2,1,0:T(8,128)S(1)}, f32[4,504,640]{2,1,0:T(8,128)}, u32[]{:S(2)}) copy-start(f32[4,504,640]{2,1,0:T(8,128)} %copy-done.13) | copy-start | bytes 15482884
  58.7 1.2 copy-start.16
  59.9 1.2 copy-start.18
  61.1 1.1 copy-start.19
  79.3 21.5 %copy-start.1 = (bf16[4,768,640]{2,1,0:T(8,128)(2,1)S(1)}, bf16[4,768,640]{2,1,0:T(8,128)(2,1)}, u32[]{:S(2)}) copy-start(bf16[4,768,640]{2,1,0:T(8,128)(2,1)} %copy-done) | copy-start | bytes 11796484
  84.1 9.3 %collective-permute-start.10 = (f32[256,128]{1,0:T(8,128)S(1)}, f32[256,128]{1,0:T(8,128)S(1)}, u32[]{:S(2)}, u32[]{:S(2)}) collective-permute-start(f32[256,128]{1,0:T(8,128)S(1)} %get-tuple-element.99), channel_id=1, source_target_pairs={{0,3},{1,4},{2,5},{3,6},{4,7},{5,8},{6,9},{7,10},{8,11},{9,12},{10... | collective-permute-start | bytes 393224 | tf_op jit(solution)/shard_map/ppermute | solution.py:385
  84.2 11.8 %collective-permute-start.11 = (f32[256,128]{1,0:T(8,128)S(1)}, f32[256,128]{1,0:T(8,128)S(1)}, u32[]{:S(2)}, u32[]{:S(2)}) collective-permute-start(f32[256,128]{1,0:T(8,128)S(1)} %get-tuple-element.100), channel_id=1, source_target_pairs={{0,31},{1,0},{2,1},{3,2},{4,3},{5,4},{6,5},{7,6},{8,7},{9,8},{10,9... | collective-permute-start | bytes 393224 | tf_op jit(solution)/shard_map/ppermute | solution.py:385
  89.6 8.9 %collective-permute-start.12 = (f32[256,128]{1,0:T(8,128)S(1)}, f32[256,128]{1,0:T(8,128)S(1)}, u32[]{:S(2)}, u32[]{:S(2)}) collective-permute-start(f32[256,128]{1,0:T(8,128)S(1)} %get-tuple-element.101), channel_id=1, source_target_pairs={{0,30},{1,31},{2,0},{3,1},{4,2},{5,3},{6,4},{7,5},{8,6},{9,7},{10,... | collective-permute-start | bytes 393224 | tf_op jit(solution)/shard_map/ppermute | solution.py:385
  90.4 18.9 %collective-permute-start.13 = (f32[256,128]{1,0:T(8,128)S(1)}, f32[256,128]{1,0:T(8,128)S(1)}, u32[]{:S(2)}, u32[]{:S(2)}) collective-permute-start(f32[256,128]{1,0:T(8,128)S(1)} %get-tuple-element.102), channel_id=1, source_target_pairs={{0,29},{1,30},{2,31},{3,0},{4,1},{5,2},{6,3},{7,4},{8,5},{9,6},{10... | collective-permute-start | bytes 393224 | tf_op jit(solution)/shard_map/ppermute | solution.py:385
  90.4 18.9 %collective-permute-start.14 = (f32[256,128]{1,0:T(8,128)S(1)}, f32[256,128]{1,0:T(8,128)S(1)}, u32[]{:S(2)}, u32[]{:S(2)}) collective-permute-start(f32[256,128]{1,0:T(8,128)S(1)} %get-tuple-element.103), channel_id=1, source_target_pairs={{0,32},{32,64},{64,96},{96,128},{128,160},{160,192},{192,224},{1,3... | collective-permute-start | bytes 393224 | tf_op jit(solution)/shard_map/ppermute | solution.py:389
  93.4 15.9 %collective-permute-start.15 = (f32[256,128]{1,0:T(8,128)S(1)}, f32[256,128]{1,0:T(8,128)S(1)}, u32[]{:S(2)}, u32[]{:S(2)}) collective-permute-start(f32[256,128]{1,0:T(8,128)S(1)} %get-tuple-element.104), channel_id=1, source_target_pairs={{32,0},{64,32},{96,64},{128,96},{160,128},{192,160},{224,192},{33,... | collective-permute-start | bytes 393224 | tf_op jit(solution)/shard_map/ppermute | solution.py:389
  96.0 13.3 %collective-permute-start.8 = (f32[256,128]{1,0:T(8,128)S(1)}, f32[256,128]{1,0:T(8,128)S(1)}, u32[]{:S(2)}, u32[]{:S(2)}) collective-permute-start(f32[256,128]{1,0:T(8,128)S(1)} %get-tuple-element.97), channel_id=1, source_target_pairs={{0,1},{1,2},{2,3},{3,4},{4,5},{5,6},{6,7},{7,8},{8,9},{9,10},{10,1... | collective-permute-start | bytes 393224 | tf_op jit(solution)/shard_map/ppermute | solution.py:385
  98.5 10.8 %collective-permute-start.9 = (f32[256,128]{1,0:T(8,128)S(1)}, f32[256,128]{1,0:T(8,128)S(1)}, u32[]{:S(2)}, u32[]{:S(2)}) collective-permute-start(f32[256,128]{1,0:T(8,128)S(1)} %get-tuple-element.98), channel_id=1, source_target_pairs={{0,2},{1,3},{2,4},{3,5},{4,6},{5,7},{6,8},{7,9},{8,10},{9,11},{10,... | collective-permute-start | bytes 393224 | tf_op jit(solution)/shard_map/ppermute | solution.py:385
  100.8 8.6 %copy-start.9 = (bf16[4,512,640]{2,1,0:T(8,128)(2,1)S(1)}, bf16[4,512,640]{2,1,0:T(8,128)(2,1)}, u32[]{:S(2)}) copy-start(bf16[4,512,640]{2,1,0:T(8,128)(2,1)} %compare_convert_fusion.1.refs_7_) | copy-start | bytes 7864324
  100.8 8.6 %copy-start.20 = (f32[4,9,9,640]{3,0,2,1:T(4,128)S(1)}, f32[4,9,9,640]{3,0,2,1:T(4,128)}, u32[]{:S(2)}) copy-start(f32[4,9,9,640]{3,0,2,1:T(4,128)} %param.21) | copy-start | bytes 2488324
  126.4 9.9 %collective-permute-start.18 = (f32[256,128]{1,0:T(8,128)S(1)}, f32[256,128]{1,0:T(8,128)S(1)}, u32[]{:S(2)}, u32[]{:S(2)}) collective-permute-start(f32[256,128]{1,0:T(8,128)S(1)} %get-tuple-element.118), channel_id=1, source_target_pairs={{0,3},{1,4},{2,5},{3,6},{4,7},{5,8},{6,9},{7,10},{8,11},{9,12},{10... | collective-permute-start | bytes 393224 | tf_op jit(solution)/shard_map/ppermute | solution.py:385
  128.4 10.6 %collective-permute-start.19 = (f32[256,128]{1,0:T(8,128)S(1)}, f32[256,128]{1,0:T(8,128)S(1)}, u32[]{:S(2)}, u32[]{:S(2)}) collective-permute-start(f32[256,128]{1,0:T(8,128)S(1)} %get-tuple-element.119), channel_id=1, source_target_pairs={{0,31},{1,0},{2,1},{3,2},{4,3},{5,4},{6,5},{7,6},{8,7},{9,8},{10,9... | collective-permute-start | bytes 393224 | tf_op jit(solution)/shard_map/ppermute | solution.py:385
  131.6 14.2 %collective-permute-start.20 = (f32[256,128]{1,0:T(8,128)S(1)}, f32[256,128]{1,0:T(8,128)S(1)}, u32[]{:S(2)}, u32[]{:S(2)}) collective-permute-start(f32[256,128]{1,0:T(8,128)S(1)} %get-tuple-element.120), channel_id=1, source_target_pairs={{0,30},{1,31},{2,0},{3,1},{4,2},{5,3},{6,4},{7,5},{8,6},{9,7},{10,... | collective-permute-start | bytes 393224 | tf_op jit(solution)/shard_map/ppermute | solution.py:385
  132.8 23.7 %collective-permute-start.16 = (f32[256,128]{1,0:T(8,128)S(1)}, f32[256,128]{1,0:T(8,128)S(1)}, u32[]{:S(2)}, u32[]{:S(2)}) collective-permute-start(f32[256,128]{1,0:T(8,128)S(1)} %get-tuple-element.116), channel_id=1, source_target_pairs={{0,1},{1,2},{2,3},{3,4},{4,5},{5,6},{6,7},{7,8},{8,9},{9,10},{10,1... | collective-permute-start | bytes 393224 | tf_op jit(solution)/shard_map/ppermute | solution.py:385
  132.8 23.7 %collective-permute-start.17 = (f32[256,128]{1,0:T(8,128)S(1)}, f32[256,128]{1,0:T(8,128)S(1)}, u32[]{:S(2)}, u32[]{:S(2)}) collective-permute-start(f32[256,128]{1,0:T(8,128)S(1)} %get-tuple-element.117), channel_id=1, source_target_pairs={{0,2},{1,3},{2,4},{3,5},{4,6},{5,7},{6,8},{7,9},{8,10},{9,11},{10,... | collective-permute-start | bytes 393224 | tf_op jit(solution)/shard_map/ppermute | solution.py:385
  136.3 20.2 %collective-permute-start.21 = (f32[256,128]{1,0:T(8,128)S(1)}, f32[256,128]{1,0:T(8,128)S(1)}, u32[]{:S(2)}, u32[]{:S(2)}) collective-permute-start(f32[256,128]{1,0:T(8,128)S(1)} %get-tuple-element.121), channel_id=1, source_target_pairs={{0,29},{1,30},{2,31},{3,0},{4,1},{5,2},{6,3},{7,4},{8,5},{9,6},{10... | collective-permute-start | bytes 393224 | tf_op jit(solution)/shard_map/ppermute | solution.py:385
  139.0 17.5 %collective-permute-start.22 = (f32[256,128]{1,0:T(8,128)S(1)}, f32[256,128]{1,0:T(8,128)S(1)}, u32[]{:S(2)}, u32[]{:S(2)}) collective-permute-start(f32[256,128]{1,0:T(8,128)S(1)} %get-tuple-element.122), channel_id=1, source_target_pairs={{0,32},{32,64},{64,96},{96,128},{128,160},{160,192},{192,224},{1,3... | collective-permute-start | bytes 393224 | tf_op jit(solution)/shard_map/ppermute | solution.py:389
  145.8 10.8 %collective-permute-start.23 = (f32[256,128]{1,0:T(8,128)S(1)}, f32[256,128]{1,0:T(8,128)S(1)}, u32[]{:S(2)}, u32[]{:S(2)}) collective-permute-start(f32[256,128]{1,0:T(8,128)S(1)} %get-tuple-element.123), channel_id=1, source_target_pairs={{32,0},{64,32},{96,64},{128,96},{160,128},{192,160},{224,192},{33,... | collective-permute-start | bytes 393224 | tf_op jit(solution)/shard_map/ppermute | solution.py:389
  156.5 12.5 %copy-start.32 = (s32[16]{0:T(128)S(1)}, s32[16]{0:T(128)}, u32[]{:S(2)}) copy-start(s32[16]{0:T(128)} %param.28) | copy-start | bytes 196
  (9 other events, 7.3 us)
